TPU v7x, 128 devices: a whole 4x4x4 slice. The times are simulated.
128 devices in a mesh: sys: 1, aux: 16 (over z, y), orb: 8 (over x, core).
Axes of the slice: x: 4, y: 4, z: 4, core: 2. Of those that a mesh axis runs over, the one named last changes fastest.
Arguments:
- aux_ints: float32 [1856, 384, 384], P(('sys', 'aux'), 'orb')
- metric: float32 [1856, 1856], P(('sys', 'aux'))
- orbitals: float32 [4, 384, 80], P('sys')
Outputs:
- output: float32 [4, 384, 384], P('sys', 'orb', 'aux')
All inputs are finite; a program needn't handle non-finite values.
Results may differ from a plain program's by a relative error of at most 0.001.
Values are sent between devices in bfloat16 or wider.
A program may use at most 1 GiB of HBM per device.

v0:
```python
import jax
import jax.numpy as jnp
from jax import lax
from jax.sharding import PartitionSpec as P

PRECISE = lax.Precision.HIGHEST


def solution(mesh):
    def local_fock(ints_blk, metric_blk, orbitals):
        m_loc = ints_blk.shape[1]
        row_start = lax.axis_index('orb') * m_loc
        half_tr = jnp.einsum('qml,dli->qmdi', ints_blk, orbitals, precision=PRECISE, preferred_element_type=jnp.float32)
        orb_rows = lax.dynamic_slice_in_dim(orbitals, row_start, m_loc, axis=1)
        gamma_part = jnp.einsum('qmdi,dmi->dq', half_tr, orb_rows, precision=PRECISE, preferred_element_type=jnp.float32)
        gamma_raw = lax.psum(gamma_part, 'orb')
        gamma_all = lax.all_gather(gamma_raw, 'aux', axis=1, tiled=True)
        gamma_fit = jnp.einsum('dq,pq->dp', gamma_all, metric_blk, precision=PRECISE, preferred_element_type=jnp.float32)
        weight_part = jnp.dot(gamma_fit, metric_blk, precision=PRECISE, preferred_element_type=jnp.float32)
        weights = lax.psum_scatter(weight_part, 'aux', scatter_dimension=1, tiled=True)
        coulomb = jnp.einsum('dq,qmn->dmn', weights, ints_blk, precision=PRECISE, preferred_element_type=jnp.float32)
        half_all = lax.all_gather(half_tr, 'aux', axis=0, tiled=True)
        fitted = jnp.einsum('pq,qmdi->pmdi', metric_blk, half_all, precision=PRECISE, preferred_element_type=jnp.float32)
        fitted_all = lax.all_gather(fitted, 'orb', axis=1, tiled=True)
        exchange = jnp.einsum('pmdi,pndi->dmn', fitted, fitted_all, precision=PRECISE, preferred_element_type=jnp.float32)
        fock_part = 2.0 * coulomb - exchange
        return lax.psum_scatter(fock_part, 'aux', scatter_dimension=2, tiled=True)

    return jax.shard_map(local_fock, mesh=mesh, in_specs=(P(('sys', 'aux'), 'orb', None), P(('sys', 'aux'), None), P('sys', None, None)), out_specs=P('sys', 'orb', 'aux'), check_vma=False)
```

profile of v0, /device:TPU:0, one launch (start us, length us, event | category | flops | bytes accessed | tf_op | source)
XLA Modules:
  0.0 1842.9 jit_solution(15056766971960007332)
XLA Ops:
  6.5 0.0 copy-start
  6.5 0.0 all-gather.4.cloned.1.call-start
  6.5 1.2 dynamic-slice_bitcast_fusion
  7.7 0.1 copy.47
  7.8 25.0 %multiply_reduce_fusion = (f32[4,116]{0,1:T(8,128)S(1)}, f32[116,48,4,80]{3,1,2,0:T(8,128)}) fusion(f32[4,80,48]{1,2,0:T(8,128)S(1)} %copy.47, f32[4,384,80]{1,2,0:T(8,128)} %param.5, f32[116,48,384]{2,1,0:T(8,128)} %param.3), kind=kOutput, calls=%fused_computation.4 | convolution fusion | flops 8213913088 | bytes 16234304 | tf_op jit(solution)/shard_map/qml,dli->qmdi/dot_general | solution.py:13
  32.8 0.0 all-gather.4.cloned.1.call-update
  32.9 0.0 copy-start.1
  32.9 0.0 all-gather.6.cloned.1.call-start
  32.9 958.8 %all-gather.4.cloned.1.call-done = f32[1856,48,4,80]{3,1,2,0:T(8,128)} async-done(((f32[116,48,4,80]{3,1,2,0:T(8,128)}), f32[1856,48,4,80]{3,1,2,0:T(8,128)}) %all-gather.4.cloned.1.call-update) | async-done | bytes 114032656 | tf_op jit(solution)/shard_map/all_gather | solution.py:22
  991.7 0.0 copy-done
  991.7 366.2 %fusion.9 = f32[116,48,4,80]{0,3,2,1:T(8,128)} fusion(f32[1856,48,4,80]{3,1,2,0:T(8,128)} %all-gather.4.cloned.1.call-done, f32[116,1856]{1,0:T(8,128)S(1)} %copy-done), kind=kOutput, calls=%fused_computation.10 | convolution fusion | flops 39683358720 | bytes 122020864 | tf_op jit(solution)/shard_map/pq,qmdi->pmdi/dot_general | solution.py:23
  1357.9 0.0 all-gather.6.cloned.1.call-update
  1357.9 0.0 all-reduce.4.cloned.1.call-start
  1358.0 0.1 copy.41
  1358.1 14.3 psum.7
  1372.4 23.1 %all-gather = f32[16,116,4]{1,2,0:T(4,128)S(1)} all-gather(f32[1,116,4]{1,2,0:T(4,128)S(1)} %bitcast.42), channel_id=1, replica_groups=mesh['sys'=1,'aux'=16,'orb'=8] {'aux'}, dimensions={0}, use_global_device_ids=true | all-gather | bytes 31552 | tf_op jit(solution)/shard_map/all_gather | solution.py:17
  1395.4 0.1 reshape.1
  1395.5 0.0 copy-done.1
  1395.5 0.6 dynamic-slice
  1396.8 0.9 fusion.25
  1397.7 0.6 fusion.26
  1398.2 72.1 %all-reduce = f32[4,1856]{1,0:T(4,128)S(1)} all-reduce(f32[4,1856]{1,0:T(4,128)S(1)} %fusion.26), channel_id=2, replica_groups=mesh['sys'=1,'aux'=16,'orb'=8] {'aux'}, use_global_device_ids=true, to_apply=%region_1.0.clone | all-reduce | flops 7424 | bytes 59392
  1470.3 9.2 fusion.4
  1479.5 158.0 %all-gather.6.cloned.1.call-done = f32[116,384,4,80]{0,3,2,1:T(8,128)} async-done(((f32[116,48,4,80]{0,3,2,1:T(8,128)}), f32[116,384,4,80]{0,3,2,1:T(8,128)}) %all-gather.6.cloned.1.call-update) | async-done | bytes 57016336 | tf_op jit(solution)/shard_map/all_gather | solution.py:24
  1637.5 109.5 %fusion.17 = f32[4,48,384]{2,1,0:T(8,128)S(1)} fusion(f32[116,384,4,80]{0,3,2,1:T(8,128)} %all-gather.6.cloned.1.call-done, f32[116,48,4,80]{0,3,2,1:T(8,128)} %fusion.9, f32[4,48,384]{2,0,1:T(4,128)S(1)} %fusion.4), kind=kOutput, calls=%fused_computation.12 | convolution fusion | flops 8210497536 | bytes 64733184 | tf_op jit(solution)/shard_map/pmdi,pndi->dmn/dot_general | solution.py:25
  1747.0 1.2 copy.31
  1748.2 0.0 all-reduce.4.cloned.1.call-update
  1748.9 85.9 %all-reduce.4.cloned.1.call-done = f32[4,48,384]{1,0,2:T(4,128)} async-done(((f32[4,48,384]{1,0,2:T(4,128)}), f32[4,48,384]{1,0,2:T(4,128)}) %all-reduce.4.cloned.1.call-update) | async-done | bytes 294928
  1834.7 0.8 constant_dynamic-slice_fusion
  1835.5 0.6 copy.32
  (1 shorter events, 0.0 us)
Async XLA Ops:
  6.5 985.2 %copy-start = (f32[116,1856]{1,0:T(8,128)S(1)}, f32[116,1856]{1,0:T(8,128)}, u32[]{:S(2)}) copy-start(f32[116,1856]{1,0:T(8,128)} %param.4) | copy-start | bytes 2583556
  6.5 985.2 %all-gather.4.cloned.1.call-start = ((), (), s32[]{:S(2)}) async-start(), calls=%async_computation | async-start | bytes 193855488 | tf_op jit(solution)/shard_map/all_gather | solution.py:22
  32.9 1362.7 %copy-start.1 = (u32[128]{0:T(128)S(1)}, u32[128]{0:T(128)}, u32[]{:S(2)}) copy-start(u32[128]{0:T(128)} %constant.17) | copy-start | bytes 1540
  32.9 1604.6 %all-gather.6.cloned.1.call-start = ((), (), s32[]{:S(2)}) async-start(), calls=%async_computation.1 | async-start | bytes 70778880 | tf_op jit(solution)/shard_map/all_gather | solution.py:24
  1357.9 476.8 %all-reduce.4.cloned.1.call-start = ((), (), s32[]{:S(2)}) async-start(), calls=%async_computation.2 | async-start | bytes 1572864
Sparse Core Ops, SparseCore 0:
  33.0 958.6 all-gather.3
  1358.1 279.4 all-gather.5
  1748.3 86.3 all-reduce.3
where the time goes:
time: 1850 us; the launch traced here: 1840 us
  waiting for transfers between devices  1200 us (65%)
  matrix products  511 us (28%)
  blocking collectives  109 us (6%)
    all_gather x1, waiting for transfers between devices, local_fock(): half_all = lax.all_gather(half_tr, 'aux', axis=0, tiled=True)  959 us
    dot_general x1, matrix products, local_fock(): jnp.einsum('pq,qmdi->pmdi', metric_blk, half_all, precision=PRECISE, pref...  366 us
    all_gather x1, waiting for transfers between devices, local_fock(): fitted_all = lax.all_gather(fitted, 'orb', axis=1, tiled=True)  158 us
    dot_general x1, matrix products, local_fock(): jnp.einsum('pmdi,pndi->dmn', fitted, fitted_all, precision=PRECISE, prefe...  109 us
    unnamed x4, waiting for transfers between devices  85.9 us
    unnamed x1, blocking collectives  72.1 us
  transfers between devices with their start and end apart: 3, of which 3 were waited for; matrix products, arithmetic and copies ran while one was open for 1% of the time, Pallas kernels for 0%

commit v1 on v0

v1 whole, which is shorter than its diff:
```python
import jax
import jax.numpy as jnp
from jax import lax
from jax.sharding import PartitionSpec as P

PRECISE = lax.Precision.HIGHEST
F32 = jnp.float32
BF16 = jnp.bfloat16


def solution(mesh):
    n_aux, n_orb = mesh.shape['aux'], mesh.shape['orb']
    chips = n_aux * n_orb // 2

    def local_fock(ints_blk, metric_blk, orbitals):
        q_loc, m_loc, n_bas = ints_blk.shape
        dens, _, n_occ = orbitals.shape
        cols = dens * n_occ // chips
        orb = lax.axis_index('orb')
        half = lax.rem(orb, 2)
        row_start = orb * m_loc
        p_half = q_loc // 2
        met_part = lax.dynamic_slice_in_dim(metric_blk, half * p_half, p_half, axis=0).astype(BF16)
        met = lax.all_gather(met_part, 'aux', axis=0, tiled=True)

        flat_orb = orbitals.transpose(1, 0, 2).reshape(n_bas, dens * n_occ)
        half_tr = jnp.einsum('qml,lc->cmq', ints_blk, flat_orb, precision=PRECISE, preferred_element_type=F32)

        send = half_tr.astype(BF16).reshape(chips, cols, 2, m_loc // 2, q_loc)
        send = send.transpose(0, 2, 1, 3, 4).reshape(2 * chips, cols, m_loc // 2, q_loc)
        recv = lax.all_to_all(send, ('aux', 'orb'), 0, 0, tiled=True)
        pair = [(i, i ^ 1) for i in range(n_orb)]
        other = lax.ppermute(recv, 'orb', pair)
        both = jnp.stack([jnp.where(half == 0, recv, other), jnp.where(half == 0, other, recv)])
        both = both.reshape(2, n_aux, n_orb, cols, m_loc // 2, q_loc)
        t0 = both.transpose(1, 5, 3, 2, 0, 4).reshape(n_aux * q_loc, cols * n_bas)

        orb_rows = lax.dynamic_slice_in_dim(flat_orb, row_start, m_loc, axis=0)
        gamma_part = (half_tr * orb_rows.T[:, :, None]).reshape(dens, n_occ * m_loc, q_loc).sum(1)
        gamma_raw = lax.psum(gamma_part, 'orb')
        gamma_all = lax.all_gather(gamma_raw, 'aux', axis=1, tiled=True)
        gamma_fit = jnp.einsum('dq,pq->dp', gamma_all, metric_blk, precision=PRECISE, preferred_element_type=F32)
        weight_part = jnp.dot(gamma_fit, metric_blk, precision=PRECISE, preferred_element_type=F32)
        weights = lax.psum_scatter(weight_part, 'aux', scatter_dimension=1, tiled=True)
        coulomb = jnp.einsum('dq,qmn->dmn', weights, ints_blk, precision=PRECISE, preferred_element_type=F32)
        coul = lax.psum_scatter(coulomb, 'aux', scatter_dimension=2, tiled=True)

        fitted = lax.dot(met, t0, preferred_element_type=F32)
        fitted = fitted.reshape(-1, cols, n_bas)
        part = jnp.einsum('pcm,pcn->mn', fitted, fitted, precision=PRECISE, preferred_element_type=F32)
        n_out = n_bas // n_aux
        part = part.reshape(n_orb, m_loc, n_aux, n_out).transpose(2, 0, 1, 3).reshape(n_aux * n_orb, m_loc, n_out)
        got = lax.all_to_all(part, ('aux', 'orb'), 0, 0, tiled=True)
        exch = got.reshape(dens, -1, m_loc, n_out).sum(1)
        return 2.0 * coul - exch

    return jax.shard_map(local_fock, mesh=mesh, in_specs=(P(('sys', 'aux'), 'orb', None), P(('sys', 'aux'), None), P('sys', None, None)), out_specs=P('sys', 'orb', 'aux'), check_vma=False)
```

time: 1850 us -> 432 us (0.23)
  waiting for transfers between devices: 1200 us -> 142 us
  matrix products: 511 us -> 63.9 us
  local copies, waits for them, and re-layouts: 4.6 us -> 59.2 us
    all_gather x2 -> x1, waiting for transfers between devices: 1120 us -> 0.01 us  [local_fock(): met = lax.all_gather(met_part, 'aux', axis=0, tiled=True)]
    dot_general x3, matrix products: 501 us -> 53.2 us  [the longest x1 19.8 us: local_fock(): fitted = lax.dot(met, t0, preferred_element_type=F32)]
    all_to_all x0 -> x2, waiting for transfers between devices: none -> 55 us  [the longest x1 55 us: local_fock(): recv = lax.all_to_all(send, ('aux', 'orb'), 0, 0, tiled=True)]
    unnamed x4 -> x3, waiting for transfers between devices: 85.9 us -> 86.8 us
  transfers between devices with their start and end apart: 3 -> 5, of which waited for: 3 -> 2; matrix products, arithmetic and copies ran while one was open for 1% -> 6% of each run, Pallas kernels for 0% -> 0%
where the time goes in v1:
time: 432 us; the launch traced here: 428 us
  waiting for transfers between devices  142 us (33%)
  blocking collectives  120 us (28%)
  matrix products  63.9 us (15%)
  local copies, waits for them, and re-layouts  59.2 us (14%)
  starting transfers between devices  16.4 us (4%)
  between operations  15.1 us (3%)
  other arithmetic  11 us (3%)
    unnamed x3, waiting for transfers between devices  86.8 us
    unnamed x1, blocking collectives  72.1 us
    all_to_all x1, waiting for transfers between devices, local_fock(): recv = lax.all_to_all(send, ('aux', 'orb'), 0, 0, tiled=True)  55 us
    all_gather x1, blocking collectives, local_fock(): gamma_all = lax.all_gather(gamma_raw, 'aux', axis=1, tiled=True)  35 us
    dot_general x1, matrix products, local_fock(): fitted = lax.dot(met, t0, preferred_element_type=F32)  19.8 us
    dot_general x1, matrix products, local_fock(): jnp.einsum('qml,lc->cmq', ints_blk, flat_orb, precision=PRECISE, preferre...  18.5 us
    dot_general x1, matrix products, local_fock(): jnp.einsum('pcm,pcn->mn', fitted, fitted, precision=PRECISE, preferred_el...  14.9 us
    reshape x1, local copies, waits for them, and re-layouts, local_fock(): t0 = both.transpose(1, 5, 3, 2, 0, 4).reshape(n_aux * q_loc, cols * n_bas)  14.7 us
  transfers between devices with their start and end apart: 5, of which 2 were waited for; matrix products, arithmetic and copies ran while one was open for 6% of the time, Pallas kernels for 0%

profile of v1, /device:TPU:0, one launch (start us, length us, event | category | flops | bytes accessed | tf_op | source)
XLA Modules:
  0.0 427.8 jit_solution(11670476382685902992)
XLA Ops:
  6.5 1.2 dynamic-slice_bitcast_fusion
  7.8 18.5 %multiply_reduce_fusion = (f32[320,116]{1,0:T(8,128)S(1)}, bf16[320,48,116]{2,0,1:T(8,128)(2,1)S(1)}) fusion(f32[320,48]{0,1:T(8,128)S(1)} %copy.35, f32[384,320,1]{0,1,2:T(8,128)} %bitcast.66, f32[116,48,384]{2,1,0:T(8,128)} %param.3), kind=kOutput, calls=%fused_computation.5 | convolution fusion | flops 8215658496 | bytes 12817408 | tf_op jit(solution)/shard_map/qml,lc->cmq/dot_general | solution.py:27
  26.3 2.5 copy.40
  28.9 2.7 copy.41
  31.5 11.7 %all-to-all-start = ((bf16[128,5,24,116]{3,2,1,0:T(8,128)(2,1)}), bf16[128,5,24,116]{3,2,1,0:T(8,128)(2,1)}, u32[]{:S(2)}, u32[]{:S(2)}) async-start(bf16[128,5,24,116]{3,2,1,0:T(8,128)(2,1)} %bitcast.58), calls=%async_computation | async-start | bytes 7864320 | tf_op jit(solution)/shard_map/all_to_all | solution.py:31
  43.3 0.8 fusion.4
  44.1 55.0 %all-to-all-done = bf16[128,5,24,116]{3,2,1,0:T(8,128)(2,1)} async-done(((bf16[128,5,24,116]{3,2,1,0:T(8,128)(2,1)}), bf16[128,5,24,116]{3,2,1,0:T(8,128)(2,1)}, u32[]{:S(2)}, u32[]{:S(2)}) %all-to-all-start) | async-done | bytes 3563552 | tf_op jit(solution)/shard_map/all_to_all | solution.py:31
  99.1 6.8 %copy.42 = bf16[128,5,24,116]{0,2,3,1:T(8,128)(2,1)} copy(bf16[128,5,24,116]{3,2,1,0:T(8,128)(2,1)} %all-to-all-done) | data formatting | bytes 7127040 | tf_op jit(solution)/shard_map/all_to_all | solution.py:31
  105.9 13.3 %psum.7 = f32[4,116]{1,0:T(4,128)S(1)} all-reduce(f32[4,116]{1,0:T(4,128)S(1)} %reduce_sum.27), channel_id=1, replica_groups=mesh['sys'=1,'aux'=16,'orb'=8] {'orb'}, use_global_device_ids=true, to_apply=%region_2.3 | all-reduce | flops 464 | bytes 3712 | tf_op jit(solution)/shard_map/psum | solution.py:40
  119.2 35.0 %all-gather = f32[16,116,4]{1,2,0:T(4,128)S(1)} all-gather(f32[1,116,4]{1,2,0:T(4,128)S(1)} %bitcast.68), channel_id=1, replica_groups=mesh['sys'=1,'aux'=16,'orb'=8] {'aux'}, dimensions={0}, use_global_device_ids=true | all-gather | bytes 31552 | tf_op jit(solution)/shard_map/all_gather | solution.py:41
  155.7 0.9 fusion.9
  157.1 72.1 %all-reduce = f32[4,1856]{1,0:T(4,128)S(1)} all-reduce(f32[4,1856]{1,0:T(4,128)S(1)} %fusion.10), channel_id=2, replica_groups=mesh['sys'=1,'aux'=16,'orb'=8] {'aux'}, use_global_device_ids=true, to_apply=%region_3.4.clone | all-reduce | flops 7424 | bytes 59392
  229.2 5.3 %reshape.44 = bf16[928,1856,1]{1,0,2:T(8,128)(2,1)} reshape(bf16[16,58,1856]{2,1,0:T(8,128)(2,1)} %all-gather.4.cloned.1.call-done) | data formatting | bytes 6889472
  234.4 6.6 %copy.43 = bf16[128,5,24,116]{3,2,1,0:T(8,128)(2,1)} copy(bf16[128,5,24,116]{0,2,3,1:T(8,128)(2,1)} %collective-permute-done) | data formatting | bytes 7127040 | tf_op jit(solution)/shard_map/ppermute | solution.py:33
  241.1 3.6 broadcast_select_fusion.1
  244.7 4.6 %copy.45 = bf16[1,16,8,5,24,116]{5,1,4,0,2,3:T(8,128)(2,1)S(1)} copy(bf16[1,16,8,5,24,116]{5,4,3,2,1,0:T(8,128)(2,1)S(1)} %bitcast.60) | data formatting | bytes 7127040 | tf_op jit(solution)/shard_map/stack | solution.py:34
  249.2 4.6 %copy.46 = bf16[1,16,8,5,24,116]{5,1,4,0,2,3:T(8,128)(2,1)S(1)} copy(bf16[1,16,8,5,24,116]{5,4,3,2,1,0:T(8,128)(2,1)S(1)} %bitcast.59) | data formatting | bytes 7127040 | tf_op jit(solution)/shard_map/stack | solution.py:34
  253.8 4.6 %maximum_bitcast_fusion = bf16[16,116,5,8,2,24]{1,0,5,4,3,2:T(8,128)(2,1)} fusion(bf16[1,16,8,5,24,116]{5,1,4,0,2,3:T(8,128)(2,1)S(1)} %copy.46, bf16[1,16,8,5,24,116]{5,1,4,0,2,3:T(8,128)(2,1)S(1)} %copy.45), kind=kLoop, calls=%fused_computation.4 | loop fusion | flops 3563520 | bytes 14254080 | tf_op jit(solution)/shard_map/transpose | solution.py:36
  258.4 14.7 %reshape.34 = bf16[1856,1920]{0,1:T(8,128)(2,1)} reshape(bf16[16,116,5,8,2,24]{1,0,5,4,3,2:T(8,128)(2,1)} %maximum_bitcast_fusion) | data formatting | bytes 14254080 | tf_op jit(solution)/shard_map/reshape | solution.py:36
  273.1 19.8 %fusion.11 = f32[928,5,384]{2,0,1:T(8,128)S(1)} fusion(bf16[928,1856,1]{1,0,2:T(8,128)(2,1)} %reshape.44, bf16[5,384,1856]{2,1,0:T(8,128)(2,1)} %bitcast.62), kind=kOutput, calls=%fused_computation.21 | convolution fusion | flops 6613893120 | bytes 17698816 | tf_op jit(solution)/shard_map/dot_general | solution.py:48
  292.9 14.9 %convolution_bitcast_fusion = f32[384,384]{0,1:T(8,128)S(1)} fusion(f32[928,5,384]{2,0,1:T(8,128)S(1)} %fusion.11), kind=kOutput, calls=%fused_computation.10 | convolution fusion | flops 8210350080 | bytes 7716864 | tf_op jit(solution)/shard_map/pcm,pcn->mn/dot_general | solution.py:50
  307.8 0.6 reshape.35
  308.4 1.4 copy.49
  309.8 3.6 reshape.51
  313.4 4.6 %all-to-all-start.1 = ((f32[128,1,1152]{2,1,0:T(1,128)}), f32[128,1,1152]{2,1,0:T(1,128)S(1)}, u32[]{:S(2)}, u32[]{:S(2)}) async-start(f32[128,1,1152]{2,1,0:T(1,128)} %reshape.51), calls=%async_computation.1 | async-start | bytes 1179648 | tf_op jit(solution)/shard_map/all_to_all | solution.py:53
  318.1 9.3 %fusion = f32[4,48,384]{2,0,1:T(4,128)S(1)} fusion(f32[116,48,384]{2,1,0:T(8,128)} %param.3, f32[4,1856]{1,0:T(4,128)S(1)} %all-reduce, u32[]{:T(128)S(6)} %multiply.1), kind=kOutput, calls=%fused_computation | convolution fusion | flops 102629376 | bytes 8849412 | tf_op jit(solution)/shard_map/dq,qmn->dmn/dot_general | solution.py:45
  327.4 1.2 copy.38
  329.3 86.7 %all-reduce.4.cloned.1.call-done = f32[4,48,384]{1,0,2:T(4,128)} async-done(((f32[4,48,384]{1,0,2:T(4,128)}), f32[4,48,384]{1,0,2:T(4,128)}) %all-reduce.4.cloned.1.call-update) | async-done | bytes 294928
  416.0 0.8 constant_dynamic-slice_fusion
  417.3 2.1 reduce.3
  419.4 0.7 reshape.52
  420.2 0.6 fusion.5
  (22 shorter events, 2.2 us)
Async XLA Ops:
  6.5 36.7 %copy-start = (f32[116,1856]{1,0:T(8,128)S(1)}, f32[116,1856]{1,0:T(8,128)}, u32[]{:S(2)}) copy-start(f32[116,1856]{1,0:T(8,128)} %param.4) | copy-start | bytes 2583556
  31.5 67.6 %all-to-all-start = ((bf16[128,5,24,116]{3,2,1,0:T(8,128)(2,1)}), bf16[128,5,24,116]{3,2,1,0:T(8,128)(2,1)}, u32[]{:S(2)}, u32[]{:S(2)}) async-start(bf16[128,5,24,116]{3,2,1,0:T(8,128)(2,1)} %bitcast.58), calls=%async_computation | async-start | bytes 7864320 | tf_op jit(solution)/shard_map/all_to_all | solution.py:31
  43.2 186.0 %all-gather.4.cloned.1.call-start = ((), (), s32[]{:S(2)}) async-start(), calls=%async_computation.2 | async-start | bytes 4177920 | tf_op jit(solution)/shard_map/all_gather | solution.py:24
  44.0 110.4 %copy-start.2 = (u32[128]{0:T(128)S(1)}, u32[128]{0:T(128)}, u32[]{:S(2)}) copy-start(u32[128]{0:T(128)} %constant.26) | copy-start | bytes 1540
  105.9 128.5 %collective-permute-start = (bf16[128,5,24,116]{0,2,3,1:T(8,128)(2,1)}, bf16[128,5,24,116]{0,2,3,1:T(8,128)(2,1)}, u32[]{:S(2)}, u32[]{:S(2)}) collective-permute-start(bf16[128,5,24,116]{0,2,3,1:T(8,128)(2,1)} %copy.42), channel_id=1, source_target_pairs={{0,1},{1,0},{2,3},{3,2},{4,5},{5,4},{6,7},{7,6},{8,9},{9,8},{10,11... | collective-permute-start | bytes 10690568 | tf_op jit(solution)/shard_map/ppermute | solution.py:33
  313.4 103.4 %all-to-all-start.1 = ((f32[128,1,1152]{2,1,0:T(1,128)}), f32[128,1,1152]{2,1,0:T(1,128)S(1)}, u32[]{:S(2)}, u32[]{:S(2)}) async-start(f32[128,1,1152]{2,1,0:T(1,128)} %reshape.51), calls=%async_computation.1 | async-start | bytes 1179648 | tf_op jit(solution)/shard_map/all_to_all | solution.py:53
  318.0 97.9 %all-reduce.4.cloned.1.call-start = ((), (), s32[]{:S(2)}) async-start(), calls=%async_computation.3 | async-start | bytes 1572864
  318.1 102.7 %copy-start.1 = (f32[116,1856]{1,0:T(8,128)S(1)}, f32[116,1856]{1,0:T(8,128)}, u32[]{:S(2)}) copy-start(f32[116,1856]{1,0:T(8,128)} %param.4) | copy-start | bytes 2583556
Sparse Core Ops, SparseCore 0:
  46.1 65.2 all-gather.3
  328.7 87.2 all-reduce.3

commit v2 on v0

v2 whole, which is shorter than its diff:
```python
import functools

import jax
import jax.numpy as jnp
from jax import lax
from jax.experimental import pallas as pl
from jax.experimental.pallas import tpu as pltpu
from jax.sharding import PartitionSpec as P

PRECISE = lax.Precision.HIGHEST
F32 = jnp.float32
BF16 = jnp.bfloat16
LANES = 128
NT = (((1,), (1,)), ((), ()))


def split3(x):
    hi = x.astype(BF16)
    rest = x - hi.astype(F32)
    mid = rest.astype(BF16)
    lo = (rest - mid.astype(F32)).astype(BF16)
    return hi, mid, lo


def split3_xla(x):
    hi = lax.reduce_precision(x, 8, 7)
    rest = x - hi
    mid = lax.reduce_precision(rest, 8, 7)
    return hi.astype(BF16), mid.astype(BF16), (rest - mid).astype(BF16)


def left_terms(x):
    hi, mid, lo = split3_xla(x)
    return jnp.concatenate([hi, hi, mid, hi, mid, lo], axis=-1)


def half_kernel(ints_hbm, orb_ref, dens_ref, out_ref, gam_ref, ints, wide, sems):
    q_loc, m_loc, n_bas = ints_hbm.shape
    n_col = orb_ref.shape[0]
    groups = m_loc // 8
    tiles = n_bas // LANES
    copies = [
        [pltpu.make_async_copy(
            ints_hbm.at[:, pl.ds(8 * g, 8), pl.ds(LANES * t, LANES)],
            ints.at[t, pl.ds(0, q_loc), pl.ds(8 * g, 8), :], sems.at[g, t]) for t in range(tiles)]
        for g in range(groups)]
    for group in copies:
        for copy in group:
            copy.start()
    ints[:, pl.ds(q_loc, LANES - q_loc)] = jnp.zeros((tiles, LANES - q_loc, m_loc, LANES), F32)
    flat = ints.reshape(tiles, LANES * m_loc, LANES)
    gam_ref[...] = jnp.zeros_like(gam_ref)

    for g in range(groups):
        for copy in copies[g]:
            copy.wait()

        def pair_step(j, carry, g=g):
            m = 8 * g + 2 * j
            rows = jnp.concatenate([
                jnp.concatenate([flat[t, pl.ds(m + u, LANES, stride=m_loc), :] for t in range(tiles)], axis=1)
                for u in range(2)], axis=0)
            hi, mid, lo = split3(rows)
            right = jnp.concatenate([hi, mid, hi, lo, mid, hi], axis=1)
            left = jnp.concatenate([orb_ref[...], dens_ref[4 * g + j]], axis=0)
            res = lax.dot_general(left, right, NT, preferred_element_type=F32)
            wide[pl.ds(m, n_col, stride=m_loc), :] = res[:n_col, :LANES]
            wide[pl.ds(m + 1, n_col, stride=m_loc), :] = res[:n_col, LANES:]
            gam_ref[...] += res[n_col:n_col + 8, :LANES] + res[n_col + 8:, LANES:]
            return carry

        lax.fori_loop(0, 4, pair_step, 0)

    def narrow(c, carry):
        rows = m_loc * 4
        out_ref[pl.ds(pl.multiple_of(c * rows, rows), rows), :] = wide[pl.ds(pl.multiple_of(c * rows, rows), rows), :].astype(BF16)
        return carry

    lax.fori_loop(0, n_col // 4, narrow, 0)


def half_transform(ints_blk, orb_terms, dens_terms):
    q_loc, m_loc, n_bas = ints_blk.shape
    n_col, depth = orb_terms.shape
    vmem = pl.BlockSpec(memory_space=pltpu.VMEM)
    return pl.pallas_call(
        half_kernel,
        out_shape=(jax.ShapeDtypeStruct((n_col * m_loc, LANES), BF16), jax.ShapeDtypeStruct((8, LANES), F32)),
        in_specs=[pl.BlockSpec(memory_space=pl.ANY), vmem, vmem],
        out_specs=(vmem, vmem),
        scratch_shapes=[
            pltpu.VMEM((n_bas // LANES, LANES, m_loc, LANES), F32),
            pltpu.VMEM((n_col * m_loc, LANES), F32),
            pltpu.SemaphoreType.DMA((m_loc // 8, n_bas // LANES)),
        ],
        compiler_params=pltpu.CompilerParams(vmem_limit_bytes=56 * 1024 * 1024),
        cost_estimate=pl.CostEstimate(flops=2 * 6 * n_col * n_bas * q_loc * m_loc, bytes_accessed=14 << 20, transcendentals=0),
        name='half_transform',
    )(ints_blk, orb_terms, dens_terms)


def fock_kernel(half_ref, own_ref, other_ref, met_ref, out_ref, fit):
    n_src, cols, m_loc, _ = own_ref.shape
    n_aux = met_ref.shape[0]
    n_x = n_src // n_aux
    rows = n_x * m_loc
    n_fit = met_ref.shape[2]
    here = pl.multiple_of(half_ref[0] * rows, rows)
    there = pl.multiple_of((1 - half_ref[0]) * rows, rows)
    tile = 256

    def col_step(c, acc):
        for src, start in ((own_ref, here), (other_ref, there)):
            for n in range(n_fit // tile):
                tot = None
                for s in range(n_aux // 2):
                    left = jnp.concatenate([src[pl.ds((2 * s + t) * n_x, n_x), c].reshape(rows, LANES) for t in range(2)], axis=1)
                    right = met_ref[pl.ds(2 * s, 2), :, pl.ds(n * tile, tile)].reshape(2 * LANES, tile)
                    part = jnp.dot(left, right, preferred_element_type=F32)
                    tot = part if tot is None else tot + part
                fit[pl.ds(start, rows), pl.ds(n * tile, tile)] = tot
        for n in range(n_fit // tile):
            hi, mid, lo = split3(fit[:, pl.ds(n * tile, tile)])
            same = lax.dot_general(hi, hi, NT, preferred_element_type=F32) + lax.dot_general(mid, mid, NT, preferred_element_type=F32)
            cross = lax.dot_general(hi, mid, NT, preferred_element_type=F32) + lax.dot_general(hi, lo, NT, preferred_element_type=F32)
            out_ref[0] += same
            out_ref[1] += cross
        return acc

    out_ref[...] = jnp.zeros_like(out_ref)
    lax.fori_loop(0, cols, col_step, 0)
    out_ref[0] += out_ref[1] + out_ref[1].T


def exchange_part(half, own, other, met):
    n_src, cols, m_loc, _ = own.shape
    n_aux, _, n_fit = met.shape
    n_bas = 2 * m_loc * n_src // n_aux
    vmem = pl.BlockSpec(memory_space=pltpu.VMEM)
    return pl.pallas_call(
        fock_kernel,
        out_shape=jax.ShapeDtypeStruct((2, n_bas, n_bas), F32),
        in_specs=[pl.BlockSpec(memory_space=pltpu.SMEM), vmem, vmem, vmem],
        out_specs=vmem,
        scratch_shapes=[pltpu.VMEM((n_bas, n_fit), F32)],
        compiler_params=pltpu.CompilerParams(vmem_limit_bytes=56 * 1024 * 1024),
        cost_estimate=pl.CostEstimate(flops=32 << 30, bytes_accessed=14 << 20, transcendentals=0),
        name='exchange_part',
    )(half, own, other, met)


def coulomb_kernel(wt_ref, ints_ref, out_ref):
    dens, q_loc = wt_ref.shape

    def q_step(q, acc):
        row = ints_ref[q]
        return tuple(acc[d] + wt_ref[d, q] * row for d in range(dens))

    acc = lax.fori_loop(0, q_loc, q_step, tuple(jnp.zeros(ints_ref.shape[1:], F32) for _ in range(dens)), unroll=4)
    for d in range(dens):
        out_ref[d] = acc[d]


def coulomb_part(weights, ints_blk):
    q_loc, m_loc, n_bas = ints_blk.shape
    dens = weights.shape[0]
    return pl.pallas_call(
        coulomb_kernel,
        grid=(m_loc // 8,),
        out_shape=jax.ShapeDtypeStruct((dens, m_loc, n_bas), F32),
        in_specs=[pl.BlockSpec(memory_space=pltpu.SMEM), pl.BlockSpec((q_loc, 8, n_bas), lambda g: (0, g, 0))],
        out_specs=pl.BlockSpec((dens, 8, n_bas), lambda g: (0, g, 0)),
        cost_estimate=pl.CostEstimate(flops=2 * dens * q_loc * m_loc * n_bas, bytes_accessed=9 << 20, transcendentals=0),
        name='coulomb_part',
    )(weights, ints_blk)


def solution(mesh):
    n_aux, n_orb = mesh.shape['aux'], mesh.shape['orb']
    n_x = n_orb // 2
    chips = n_aux * n_x
    mesh4 = jax.sharding.Mesh(mesh.devices.reshape(1, n_aux, n_x, 2), ('sys', 'aux', 'x', 'core'))

    def local_fock(ints_blk, metric_blk, orbitals):
        q_loc, m_loc, n_bas = ints_blk.shape
        dens, _, n_occ = orbitals.shape
        cols = dens * n_occ // chips
        half = lax.axis_index('core')
        orb = lax.axis_index('x') * 2 + half
        n_fit = n_bas * 0 + 1024
        met_pad = jnp.pad(metric_blk, ((0, LANES - q_loc), (0, 2 * n_fit - metric_blk.shape[1])))
        met_part = lax.dynamic_slice_in_dim(met_pad, half * n_fit, n_fit, axis=1).astype(BF16)
        met = lax.all_gather(met_part, 'aux', axis=0)

        orb_rows = lax.dynamic_slice_in_dim(orbitals, orb * m_loc, m_loc, axis=1)
        dens_rows = jnp.einsum('dmi,dli->mdl', orb_rows, orbitals, precision=PRECISE, preferred_element_type=F32)
        dens_rows = jnp.pad(dens_rows, ((0, 0), (0, 8 - dens), (0, 0))).reshape(m_loc // 2, 16, n_bas)
        orb_cols = orbitals.transpose(0, 2, 1).reshape(dens * n_occ, n_bas)
        half_tr, gamma = half_transform(ints_blk, left_terms(orb_cols), left_terms(dens_rows))

        gamma = jnp.broadcast_to(gamma[:dens][None], (2 * chips, dens, LANES))
        gamma_all = lax.all_to_all(gamma, ('aux', 'x', 'core'), 0, 0, tiled=True)
        own = lax.all_to_all(half_tr.reshape(chips, cols, m_loc, LANES), ('aux', 'x'), 0, 0, tiled=True)
        other = lax.ppermute(own, 'core', [(0, 1), (1, 0)])

        gamma_raw = gamma_all.reshape(n_aux, n_orb, dens, LANES).sum(1)[:, :, :q_loc].transpose(1, 0, 2).reshape(dens, n_aux * q_loc)
        gamma_fit = jnp.einsum('dq,pq->dp', gamma_raw, metric_blk, precision=PRECISE, preferred_element_type=F32)
        fit_all = lax.all_to_all(jnp.broadcast_to(gamma_fit[None], (n_aux, dens, q_loc)), 'aux', 0, 0, tiled=True)
        fit_all = fit_all.transpose(1, 0, 2).reshape(dens, n_aux * q_loc)
        weights = jnp.einsum('dp,qp->dq', fit_all, metric_blk, precision=PRECISE, preferred_element_type=F32)
        coulomb = coulomb_part(weights, ints_blk)
        n_out = n_bas // n_aux
        coul = coulomb.reshape(dens, m_loc, n_aux, n_out).transpose(2, 0, 1, 3)
        coul = lax.all_to_all(coul, 'aux', 0, 0, tiled=True).sum(0)

        part = exchange_part(half.reshape(1).astype(jnp.int32), own, other, met)[0]
        part = part.reshape(2, n_x, m_loc, 2, n_x, 2, n_out).transpose(4, 3, 5, 1, 0, 2, 6).reshape(2 * chips, m_loc, n_out)
        got = lax.all_to_all(part, ('aux', 'x', 'core'), 0, 0, tiled=True)
        exch = got.reshape(dens, -1, m_loc, n_out).sum(1)
        return 2.0 * coul - exch

    return jax.shard_map(
        local_fock, mesh=mesh4,
        in_specs=(P(('sys', 'aux'), ('x', 'core'), None), P(('sys', 'aux'), None), P('sys', None, None)),
        out_specs=P('sys', ('x', 'core'), 'aux'), check_vma=False)
```

time: 1850 us -> 215 us (0.12)
  waiting for transfers between devices: 1200 us -> 11.8 us
  matrix products: 511 us -> 2.9 us
  Pallas kernels: 0 us -> 57.4 us
    all_gather x2 -> x1, waiting for transfers between devices: 1120 us -> 0.02 us  [local_fock(): met = lax.all_gather(met_part, 'aux', axis=0)]
    dot_general x6 -> x3, matrix products: 511 us -> 2.9 us  [the longest x1 1.46 us: local_fock(): jnp.einsum('dp,qp->dq', fit_all, metric_blk, precision=PRECISE, preferred...]
    all_to_all x0 -> x3, blocking collectives: none -> 96.2 us  [the longest x1 68.3 us: local_fock(): lax.all_to_all(half_tr.reshape(chips, cols, m_loc, LANES), ('aux', 'x'),...]
    unnamed x4 -> x1, waiting for transfers between devices: 85.9 us -> 0.02 us
    unnamed x1 -> x0, blocking collectives: 72.1 us -> none
    pallas_call x0 -> x3, Pallas kernels: none -> 57.4 us  [the longest x1 25.5 us: half_transform(): pl.pallas_call(half_kernel, out_shape=(jax.ShapeDtypeStruct((n_col * m_lo...]
    all_gather x1 -> x0, blocking collectives: 23.1 us -> none  [local_fock(): gamma_all = lax.all_gather(gamma_raw, 'aux', axis=1, tiled=True)]
  transfers between devices with their start and end apart: 3 -> 4, of which waited for: 3 -> 1; matrix products, arithmetic and copies ran while one was open for 1% -> 7% of each run, Pallas kernels for 0% -> 27%
where the time goes in v2:
time: 215 us; the launch traced here: 214 us
  blocking collectives  96.2 us (45%)
  Pallas kernels  57.4 us (27%)
  local copies, waits for them, and re-layouts  14.3 us (7%)
  between operations  13.7 us (6%)
  starting transfers between devices  12.7 us (6%)
  waiting for transfers between devices  11.8 us (5%)
  other arithmetic  4.75 us (2%)
  matrix products  2.9 us (1%)
    all_to_all x1, blocking collectives, local_fock(): lax.all_to_all(half_tr.reshape(chips, cols, m_loc, LANES), ('aux', 'x'),...  68.3 us
    pallas_call x1, Pallas kernels, half_transform(): pl.pallas_call(half_kernel, out_shape=(jax.ShapeDtypeStruct((n_col * m_lo...  25.5 us
    pallas_call x1, Pallas kernels, exchange_part(): pl.pallas_call(fock_kernel, out_shape=jax.ShapeDtypeStruct((2, n_bas, n_b...  24.1 us
    all_to_all x1, blocking collectives, local_fock(): gamma_all = lax.all_to_all(gamma, ('aux', 'x', 'core'), 0, 0, tiled=True)  17.5 us
    all_to_all x1, waiting for transfers between devices, local_fock(): got = lax.all_to_all(part, ('aux', 'x', 'core'), 0, 0, tiled=True)  11.7 us
    all_to_all x1, blocking collectives, local_fock(): lax.all_to_all(jnp.broadcast_to(gamma_fit[None], (n_aux, dens, q_loc)), '...  10.4 us
    all_to_all x1, starting transfers between devices, local_fock(): got = lax.all_to_all(part, ('aux', 'x', 'core'), 0, 0, tiled=True)  8.77 us
    pallas_call x1, Pallas kernels, coulomb_part(): pl.pallas_call(coulomb_kernel, grid=(m_loc // 8,), out_shape=jax.ShapeDty...  7.71 us
  transfers between devices with their start and end apart: 4, of which 1 were waited for; matrix products, arithmetic and copies ran while one was open for 7% of the time, Pallas kernels for 27%

profile of v2, /device:TPU:0, one launch (start us, length us, event | category | flops | bytes accessed | tf_op | source)
XLA Modules:
  0.0 213.7 jit_solution(11088149799150864042)
XLA Ops:
  6.5 1.8 fusion.1
  8.4 0.1 fusion.2
  8.5 0.6 convolution_bitcast_fusion
  9.1 0.1 copy.50
  9.8 0.1 fusion.3.dens_ref
  10.0 1.2 copy-done.2
  11.2 1.1 copy-done.3
  12.3 25.5 %half_transform.1 = (bf16[15360,128]{1,0:T(8,128)(2,1)}, f32[8,128]{1,0:T(8,128)}) custom-call(f32[116,48,384]{2,1,0:T(8,128)} %ints_ref.1, bf16[320,2304]{1,0:T(8,128)(2,1)} %copy-done.3, bf16[24,16,2304]{2,1,0:T(8,128)(2,1)} %copy-done.2), custom_call_target="tpu_custom_call" | custom-call | flops 8210350080 | bytes 14680064 | tf_op jit(solution)/shard_map/half_transform/pallas_call | solution.py:86
  37.9 68.3 %all_to_all.25.own_ref = bf16[64,5,48,128]{3,2,1,0:T(8,128)(2,1)} all-to-all(bf16[64,5,48,128]{3,2,1,0:T(8,128)(2,1)} %bitcast.74), channel_id=1, replica_groups=mesh['sys'=1,'aux'=16,'x'=4,'core'=2] {'aux','x'}, dimensions={0} | all-to-all | bytes 7864320 | tf_op jit(solution)/shard_map/all_to_all | solution.py:203
  106.2 0.2 collective-permute-start
  106.4 17.5 %all_to_all.26 = f32[128,4,128]{2,1,0:T(4,128)S(1)} all-to-all(f32[128,4,128]{2,1,0:T(4,128)S(1)} %broadcast_in_dim.4), channel_id=1, replica_groups=mesh['sys'=1,'aux'=16,'x'=4,'core'=2] {'aux','x','core'}, dimensions={0} | all-to-all | bytes 524288 | tf_op jit(solution)/shard_map/all_to_all | solution.py:202
  124.1 0.9 fusion.8
  125.0 10.4 %all_to_all.27 = f32[16,4,116]{2,1,0:T(4,128)S(1)} all-to-all(f32[16,4,116]{2,1,0:T(4,128)S(1)} %broadcast_in_dim.5), channel_id=1, replica_groups=mesh['sys'=1,'aux'=16,'x'=4,'core'=2] {'aux'}, dimensions={0} | all-to-all | bytes 59392 | tf_op jit(solution)/shard_map/all_to_all | solution.py:208
  135.5 1.5 fusion.9.wt_ref
  136.9 7.7 %coulomb_part.1 = f32[4,48,384]{2,1,0:T(8,128)} custom-call(f32[4,116]{1,0:T(4,128)} %fusion.9.wt_ref, f32[116,48,384]{2,1,0:T(8,128)} %ints_ref.1), custom_call_target="tpu_custom_call" | custom-call | flops 17104896 | bytes 9437184 | tf_op jit(solution)/shard_map/coulomb_part/pallas_call | solution.py:167
  144.6 1.2 copy.41
  146.0 1.5 reshape.45
  147.4 3.7 %all-to-all-start.2 = ((f32[16,1,4608]{2,1,0:T(1,128)}), f32[16,1,4608]{2,1,0:T(1,128)S(1)}, u32[]{:S(2)}, u32[]{:S(2)}) async-start(f32[16,1,4608]{2,1,0:T(1,128)} %reshape.45), calls=%async_computation.2 | async-start | bytes 589824 | tf_op jit(solution)/shard_map/all_to_all | solution.py:214
  151.2 24.1 %exchange_part.1 = f32[2,384,384]{2,1,0:T(8,128)} custom-call(s32[1]{0:T(128)} %bitcast.10.half_ref, bf16[64,5,48,128]{3,2,1,0:T(8,128)(2,1)} %all_to_all.25.own_ref, bf16[64,5,48,128]{3,2,1,0:T(8,128)(2,1)} %collective-permute-done.other_ref, bf16[16,128,1024]{2,1,0:T(8,128)(2,1)} %bitcast.78), custom_call_target="tpu_custom_call" | custom-call | flops 34359738368 | bytes 14680064 | tf_op jit(solution)/shard_map/exchange_part/pallas_call | solution.py:140
  175.3 1.1 slice.13
  176.4 0.2 copy.43
  176.7 1.3 reshape_squeeze.3
  178.0 0.3 copy.44
  178.3 2.4 %reshape.43 = f32[128,1,1152]{2,1,0:T(1,128)} reshape(f32[128,24,48]{2,1,0:T(8,128)S(1)} %bitcast.73) | data formatting | bytes 1179648
  180.6 8.8 %all-to-all-start.4 = ((f32[128,1,1152]{2,1,0:T(1,128)}), f32[128,1,1152]{2,1,0:T(1,128)S(1)}, u32[]{:S(2)}, u32[]{:S(2)}) async-start(f32[128,1,1152]{2,1,0:T(1,128)} %reshape.43), calls=%async_computation.4 | async-start | bytes 1179648 | tf_op jit(solution)/shard_map/all_to_all | solution.py:218
  189.4 0.5 broadcast.6
  189.9 1.3 reduce.1
  191.3 0.3 reshape.46
  191.7 11.7 %all-to-all-done.4 = f32[128,1,1152]{2,1,0:T(1,128)S(1)} async-done(((f32[128,1,1152]{2,1,0:T(1,128)}), f32[128,1,1152]{2,1,0:T(1,128)S(1)}, u32[]{:S(2)}, u32[]{:S(2)}) %all-to-all-start.4) | async-done | bytes 589856 | tf_op jit(solution)/shard_map/all_to_all | solution.py:218
  203.4 2.0 reduce
  205.4 0.7 reshape.44
  206.2 0.6 multiply_subtract_fusion
  (37 shorter events, 1.2 us)
Async XLA Ops:
  6.5 1.9 copy-start.1
  6.5 144.7 %all-gather.3.cloned.1.call-start = ((), (), s32[]{:S(2)}) async-start(), calls=%async_computation.5 | async-start | bytes 4456448 | tf_op jit(solution)/shard_map/all_gather | solution.py:193
  10.0 1.2 copy-start.2
  11.2 1.1 copy-start.3
  37.9 68.5 %copy-start.4 = (f32[8,128]{1,0:T(8,128)S(1)}, f32[8,128]{1,0:T(8,128)}, u32[]{:S(2)}) copy-start(f32[8,128]{1,0:T(8,128)} %get-tuple-element.7) | copy-start | bytes 12292
  106.2 17.9 %copy-start = (f32[116,1856]{1,0:T(8,128)S(1)}, f32[116,1856]{1,0:T(8,128)}, u32[]{:S(2)}) copy-start(f32[116,1856]{1,0:T(8,128)} %param.4) | copy-start | bytes 2583556
  106.2 45.0 %collective-permute-start = (bf16[64,5,48,128]{3,2,1,0:T(8,128)(2,1)}, bf16[64,5,48,128]{3,2,1,0:T(8,128)(2,1)}, u32[]{:S(2)}, u32[]{:S(2)}) collective-permute-start(bf16[64,5,48,128]{3,2,1,0:T(8,128)(2,1)} %all_to_all.25.own_ref), channel_id=1, source_target_pairs={{0,1},{1,0},{2,3},{3,2},{4,5},{5,4},{6,7},{7,6},{8,9},{9,8},{10,11... | collective-permute-start | bytes 11796488 | tf_op jit(solution)/shard_map/ppermute | solution.py:204
  147.4 33.2 %all-to-all-start.2 = ((f32[16,1,4608]{2,1,0:T(1,128)}), f32[16,1,4608]{2,1,0:T(1,128)S(1)}, u32[]{:S(2)}, u32[]{:S(2)}) async-start(f32[16,1,4608]{2,1,0:T(1,128)} %reshape.45), calls=%async_computation.2 | async-start | bytes 589824 | tf_op jit(solution)/shard_map/all_to_all | solution.py:214
  180.6 22.8 %all-to-all-start.4 = ((f32[128,1,1152]{2,1,0:T(1,128)}), f32[128,1,1152]{2,1,0:T(1,128)S(1)}, u32[]{:S(2)}, u32[]{:S(2)}) async-start(f32[128,1,1152]{2,1,0:T(1,128)} %reshape.43), calls=%async_computation.4 | async-start | bytes 1179648 | tf_op jit(solution)/shard_map/all_to_all | solution.py:218
Sparse Core Ops, SparseCore 0:
  9.5 84.2 all-gather.2

commit v3 on v2

--- a/solution.py
+++ b/solution.py
@@ -99,54 +99,92 @@
     )(ints_blk, orb_terms, dens_terms)
 
 
-def fock_kernel(half_ref, own_ref, other_ref, met_ref, out_ref, fit):
-    n_src, cols, m_loc, _ = own_ref.shape
-    n_aux = met_ref.shape[0]
+def fock_kernel(send_ref, met_ref, out_ref, own, other, fit, send_sem, recv_sem, pair_send, pair_recv):
+    cols, n_src, m_loc, _ = own.shape
+    n_aux, _, n_fit = met_ref.shape
     n_x = n_src // n_aux
     rows = n_x * m_loc
-    n_fit = met_ref.shape[2]
-    here = pl.multiple_of(half_ref[0] * rows, rows)
-    there = pl.multiple_of((1 - half_ref[0]) * rows, rows)
     tile = 256
-
-    def col_step(c, acc):
-        for src, start in ((own_ref, here), (other_ref, there)):
-            for n in range(n_fit // tile):
-                tot = None
-                for s in range(n_aux // 2):
-                    left = jnp.concatenate([src[pl.ds((2 * s + t) * n_x, n_x), c].reshape(rows, LANES) for t in range(2)], axis=1)
-                    right = met_ref[pl.ds(2 * s, 2), :, pl.ds(n * tile, tile)].reshape(2 * LANES, tile)
-                    part = jnp.dot(left, right, preferred_element_type=F32)
-                    tot = part if tot is None else tot + part
-                fit[pl.ds(start, rows), pl.ds(n * tile, tile)] = tot
+    aux, x, core = lax.axis_index('aux'), lax.axis_index('x'), lax.axis_index('core')
+    z, y = aux // 4, lax.rem(aux, 4)
+    me = aux * n_x + x
+    here = pl.multiple_of(core * rows, rows)
+    there = pl.multiple_of((1 - core) * rows, rows)
+
+    def send_col(c, carry):
+        def send_one(k, carry):
+            to_aux = lax.rem(z + k // 16, 4) * 4 + lax.rem(y + lax.rem(k // 4, 4), 4)
+            to_x = lax.rem(x + lax.rem(k, 4), 4)
+            pltpu.make_async_remote_copy(
+                send_ref.at[to_aux * n_x + to_x, c], own.at[c, me], send_sem.at[c], recv_sem.at[c],
+                device_id={'aux': to_aux, 'x': to_x}, device_id_type=pl.DeviceIdType.MESH).start()
+            return carry
+
+        return lax.fori_loop(1, n_src, send_one, carry)
+
+    lax.fori_loop(0, cols, send_col, 0)
+    for c in range(cols):
+        own[c, me] = send_ref[me, c]
+    out_ref[...] = jnp.zeros_like(out_ref)
+
+    def fitted(src, c, start):
+        for n in range(n_fit // tile):
+            tot = None
+            for s in range(n_aux // 2):
+                left = jnp.concatenate([src[c, pl.ds((2 * s + t) * n_x, n_x)].reshape(rows, LANES) for t in range(2)], axis=1)
+                right = met_ref[pl.ds(2 * s, 2), :, pl.ds(n * tile, tile)].reshape(2 * LANES, tile)
+                part = jnp.dot(left, right, preferred_element_type=F32)
+                tot = part if tot is None else tot + part
+            fit[pl.ds(start, rows), pl.ds(n * tile, tile)] = tot
+
+    def col_step(c, carry):
+        got = own.at[c, pl.ds(1, n_src - 1)]
+        pltpu.make_async_copy(got, got, recv_sem.at[c]).wait()
+        swap = pltpu.make_async_remote_copy(
+            own.at[c], other.at[c], pair_send.at[c], pair_recv.at[c],
+            device_id={'core': 1 - core}, device_id_type=pl.DeviceIdType.MESH)
+        swap.start()
+        fitted(own, c, here)
+        swap.wait()
+        fitted(other, c, there)
         for n in range(n_fit // tile):
             hi, mid, lo = split3(fit[:, pl.ds(n * tile, tile)])
             same = lax.dot_general(hi, hi, NT, preferred_element_type=F32) + lax.dot_general(mid, mid, NT, preferred_element_type=F32)
             cross = lax.dot_general(hi, mid, NT, preferred_element_type=F32) + lax.dot_general(hi, lo, NT, preferred_element_type=F32)
             out_ref[0] += same
             out_ref[1] += cross
-        return acc
-
-    out_ref[...] = jnp.zeros_like(out_ref)
+        return carry
+
     lax.fori_loop(0, cols, col_step, 0)
     out_ref[0] += out_ref[1] + out_ref[1].T
-
-
-def exchange_part(half, own, other, met):
-    n_src, cols, m_loc, _ = own.shape
+    for c in range(cols):
+        sent = own.at[c, pl.ds(1, n_src - 1)]
+        pltpu.make_async_copy(sent, sent, send_sem.at[c]).wait()
+
+
+def exchange_part(send, met):
+    n_src, cols, m_loc, _ = send.shape
     n_aux, _, n_fit = met.shape
     n_bas = 2 * m_loc * n_src // n_aux
     vmem = pl.BlockSpec(memory_space=pltpu.VMEM)
     return pl.pallas_call(
         fock_kernel,
         out_shape=jax.ShapeDtypeStruct((2, n_bas, n_bas), F32),
-        in_specs=[pl.BlockSpec(memory_space=pltpu.SMEM), vmem, vmem, vmem],
+        in_specs=[vmem, vmem],
         out_specs=vmem,
-        scratch_shapes=[pltpu.VMEM((n_bas, n_fit), F32)],
-        compiler_params=pltpu.CompilerParams(vmem_limit_bytes=56 * 1024 * 1024),
+        scratch_shapes=[
+            pltpu.VMEM((cols, n_src, m_loc, LANES), BF16),
+            pltpu.VMEM((cols, n_src, m_loc, LANES), BF16),
+            pltpu.VMEM((n_bas, n_fit), F32),
+            pltpu.SemaphoreType.DMA((cols,)),
+            pltpu.SemaphoreType.DMA((cols,)),
+            pltpu.SemaphoreType.DMA((cols,)),
+            pltpu.SemaphoreType.DMA((cols,)),
+        ],
+        compiler_params=pltpu.CompilerParams(vmem_limit_bytes=56 * 1024 * 1024, has_side_effects=True),
         cost_estimate=pl.CostEstimate(flops=32 << 30, bytes_accessed=14 << 20, transcendentals=0),
         name='exchange_part',
-    )(half, own, other, met)
+    )(send, met)
 
 
 def coulomb_kernel(wt_ref, ints_ref, out_ref):
@@ -200,8 +238,6 @@
 
         gamma = jnp.broadcast_to(gamma[:dens][None], (2 * chips, dens, LANES))
         gamma_all = lax.all_to_all(gamma, ('aux', 'x', 'core'), 0, 0, tiled=True)
-        own = lax.all_to_all(half_tr.reshape(chips, cols, m_loc, LANES), ('aux', 'x'), 0, 0, tiled=True)
-        other = lax.ppermute(own, 'core', [(0, 1), (1, 0)])
 
         gamma_raw = gamma_all.reshape(n_aux, n_orb, dens, LANES).sum(1)[:, :, :q_loc].transpose(1, 0, 2).reshape(dens, n_aux * q_loc)
         gamma_fit = jnp.einsum('dq,pq->dp', gamma_raw, metric_blk, precision=PRECISE, preferred_element_type=F32)
@@ -213,7 +249,7 @@
         coul = coulomb.reshape(dens, m_loc, n_aux, n_out).transpose(2, 0, 1, 3)
         coul = lax.all_to_all(coul, 'aux', 0, 0, tiled=True).sum(0)
 
-        part = exchange_part(half.reshape(1).astype(jnp.int32), own, other, met)[0]
+        part = exchange_part(half_tr.reshape(chips, cols, m_loc, LANES), met)[0]
         part = part.reshape(2, n_x, m_loc, 2, n_x, 2, n_out).transpose(4, 3, 5, 1, 0, 2, 6).reshape(2 * chips, m_loc, n_out)
         got = lax.all_to_all(part, ('aux', 'x', 'core'), 0, 0, tiled=True)
         exch = got.reshape(dens, -1, m_loc, n_out).sum(1)

time: 215 us -> 196 us (0.912)
  blocking collectives: 96.2 us -> 32.1 us
  Pallas kernels: 57.4 us -> 106 us
  starting transfers between devices: 12.7 us -> 8.16 us
    all_to_all x1 -> x0, blocking collectives: 68.3 us -> none  [local_fock(): lax.all_to_all(half_tr.reshape(chips, cols, m_loc, LANES), ('aux', 'x'),...]
    pallas_call x1, Pallas kernels: 24.1 us -> 73.1 us  [exchange_part(): pl.pallas_call(fock_kernel, out_shape=jax.ShapeDtypeStruct((2, n_bas, n_b...]
    all_to_all x1, blocking collectives: 17.5 us -> 21.7 us  [local_fock(): gamma_all = lax.all_to_all(gamma, ('aux', 'x', 'core'), 0, 0, tiled=True)]
    all_to_all x1, starting transfers between devices: 8.77 us -> 4.62 us  [local_fock(): got = lax.all_to_all(part, ('aux', 'x', 'core'), 0, 0, tiled=True)]
    unnamed x20 -> x18, local copies, waits for them, and re-layouts: 7.47 us -> 7.29 us
  transfers between devices with their start and end apart: 4 -> 3, of which waited for: 1 -> 1; matrix products, arithmetic and copies ran while one was open for 7% -> 7% of each run, Pallas kernels for 27% -> 55%
where the time goes in v3:
time: 196 us; the launch traced here: 195 us
  Pallas kernels  106 us (54%)
  blocking collectives  32.1 us (16%)
  local copies, waits for them, and re-layouts  14.9 us (8%)
  between operations  13.7 us (7%)
  waiting for transfers between devices  11.8 us (6%)
  starting transfers between devices  8.16 us (4%)
  other arithmetic  4.75 us (2%)
  matrix products  2.9 us (1%)
    pallas_call x1, Pallas kernels, exchange_part(): pl.pallas_call(fock_kernel, out_shape=jax.ShapeDtypeStruct((2, n_bas, n_b...  73.1 us
    pallas_call x1, Pallas kernels, half_transform(): pl.pallas_call(half_kernel, out_shape=(jax.ShapeDtypeStruct((n_col * m_lo...  25.4 us
    all_to_all x1, blocking collectives, local_fock(): gamma_all = lax.all_to_all(gamma, ('aux', 'x', 'core'), 0, 0, tiled=True)  21.7 us
    all_to_all x1, waiting for transfers between devices, local_fock(): got = lax.all_to_all(part, ('aux', 'x', 'core'), 0, 0, tiled=True)  11.7 us
    all_to_all x1, blocking collectives, local_fock(): lax.all_to_all(jnp.broadcast_to(gamma_fit[None], (n_aux, dens, q_loc)), '...  10.4 us
    pallas_call x1, Pallas kernels, coulomb_part(): pl.pallas_call(coulomb_kernel, grid=(m_loc // 8,), out_shape=jax.ShapeDty...  7.73 us
    unnamed x18, local copies, waits for them, and re-layouts  7.29 us
    all_to_all x1, starting transfers between devices, local_fock(): got = lax.all_to_all(part, ('aux', 'x', 'core'), 0, 0, tiled=True)  4.62 us
  transfers between devices with their start and end apart: 3, of which 1 were waited for; matrix products, arithmetic and copies ran while one was open for 7% of the time, Pallas kernels for 55%

profile of v3, /device:TPU:0, one launch (start us, length us, event | category | flops | bytes accessed | tf_op | source)
XLA Modules:
  0.0 194.6 jit_solution(7850554006659992516)
XLA Ops:
  6.5 1.8 fusion.1
  8.4 0.6 convolution_bitcast_fusion
  9.0 0.1 copy.50
  9.2 0.1 fusion.2
  9.8 0.9 copy-done.3
  10.8 0.1 fusion.3.dens_ref
  10.9 1.3 copy-done.2
  12.2 25.4 %half_transform.1 = (bf16[15360,128]{1,0:T(8,128)(2,1)}, f32[8,128]{1,0:T(8,128)}) custom-call(f32[116,48,384]{2,1,0:T(8,128)} %ints_ref.1, bf16[320,2304]{1,0:T(8,128)(2,1)} %copy-done.3, bf16[24,16,2304]{2,1,0:T(8,128)(2,1)} %copy-done.2), custom_call_target="tpu_custom_call" | custom-call | flops 8210350080 | bytes 14680064 | tf_op jit(solution)/shard_map/half_transform/pallas_call | solution.py:86
  37.7 0.8 slice.9
  38.5 21.7 %all_to_all.20 = f32[128,4,128]{2,1,0:T(4,128)S(1)} all-to-all(f32[128,4,128]{2,1,0:T(4,128)S(1)} %broadcast_in_dim.4), channel_id=1, replica_groups=mesh['sys'=1,'aux'=16,'x'=4,'core'=2] {'aux','x','core'}, dimensions={0} | all-to-all | bytes 524288 | tf_op jit(solution)/shard_map/all_to_all | solution.py:240
  60.4 0.9 fusion.8
  61.3 10.4 %all_to_all.21 = f32[16,4,116]{2,1,0:T(4,128)S(1)} all-to-all(f32[16,4,116]{2,1,0:T(4,128)S(1)} %broadcast_in_dim.5), channel_id=1, replica_groups=mesh['sys'=1,'aux'=16,'x'=4,'core'=2] {'aux'}, dimensions={0} | all-to-all | bytes 59392 | tf_op jit(solution)/shard_map/all_to_all | solution.py:244
  71.7 1.5 fusion.9.wt_ref
  73.2 7.7 %coulomb_part.1 = f32[4,48,384]{2,1,0:T(8,128)} custom-call(f32[4,116]{1,0:T(4,128)} %fusion.9.wt_ref, f32[116,48,384]{2,1,0:T(8,128)} %ints_ref.1), custom_call_target="tpu_custom_call" | custom-call | flops 17104896 | bytes 9437184 | tf_op jit(solution)/shard_map/coulomb_part/pallas_call | solution.py:205
  80.9 1.2 copy.41
  82.2 1.5 reshape.41
  83.7 3.5 %all-to-all-start.2 = ((f32[16,1,4608]{2,1,0:T(1,128)}), f32[16,1,4608]{2,1,0:T(1,128)S(1)}, u32[]{:S(2)}, u32[]{:S(2)}) async-start(f32[16,1,4608]{2,1,0:T(1,128)} %reshape.41), calls=%async_computation.2 | async-start | bytes 589824 | tf_op jit(solution)/shard_map/all_to_all | solution.py:250
  87.3 73.1 %exchange_part.1 = f32[2,384,384]{2,1,0:T(8,128)} custom-call(bf16[64,5,48,128]{3,2,1,0:T(8,128)(2,1)} %bitcast.77, bf16[16,128,1024]{2,1,0:T(8,128)(2,1)} %bitcast.76), custom_call_target="tpu_custom_call" | custom-call | flops 34359738368 | bytes 14680064 | tf_op jit(solution)/shard_map/exchange_part/pallas_call | solution.py:170
  160.4 1.1 slice-done
  161.5 0.2 copy.43
  161.7 1.3 reshape_squeeze.3
  163.0 0.3 copy.44
  163.3 2.4 %reshape.39 = f32[128,1,1152]{2,1,0:T(1,128)} reshape(f32[128,24,48]{2,1,0:T(8,128)S(1)} %bitcast.72) | data formatting | bytes 1179648
  165.7 4.6 %all-to-all-start.3 = ((f32[128,1,1152]{2,1,0:T(1,128)}), f32[128,1,1152]{2,1,0:T(1,128)S(1)}, u32[]{:S(2)}, u32[]{:S(2)}) async-start(f32[128,1,1152]{2,1,0:T(1,128)} %reshape.39), calls=%async_computation.3 | async-start | bytes 1179648 | tf_op jit(solution)/shard_map/all_to_all | solution.py:254
  170.3 0.5 broadcast.6
  170.8 1.3 reduce.1
  172.1 0.3 reshape.42
  172.6 11.7 %all-to-all-done.3 = f32[128,1,1152]{2,1,0:T(1,128)S(1)} async-done(((f32[128,1,1152]{2,1,0:T(1,128)}), f32[128,1,1152]{2,1,0:T(1,128)S(1)}, u32[]{:S(2)}, u32[]{:S(2)}) %all-to-all-start.3) | async-done | bytes 589856 | tf_op jit(solution)/shard_map/all_to_all | solution.py:254
  184.3 2.0 %reduce = f32[128,1152]{1,0:T(8,128)S(1)} reduce(f32[128,1,1152]{2,1,0:T(1,128)S(1)} %all-to-all-done.3, f32[]{:T(128)} %broadcast.6), dimensions={1}, to_apply=%all_to_all.15.reduce_sub_computation | reduce | bytes 1179652 | tf_op jit(solution)/shard_map/all_to_all | solution.py:254
  186.3 0.7 reshape.40
  187.0 0.1 bitcast_reduce_fusion
  187.1 0.6 multiply_subtract_fusion
  (33 shorter events, 1.1 us)
Async XLA Ops:
  6.5 1.9 copy-start.1
  6.5 80.7 %all-gather.3.cloned.1.call-start = ((), (), s32[]{:S(2)}) async-start(), calls=%async_computation.4 | async-start | bytes 4456448 | tf_op jit(solution)/shard_map/all_gather | solution.py:231
  9.6 1.1 copy-start.3
  10.9 1.3 copy-start.2
  37.7 22.7 %copy-start = (f32[116,1856]{1,0:T(8,128)S(1)}, f32[116,1856]{1,0:T(8,128)}, u32[]{:S(2)}) copy-start(f32[116,1856]{1,0:T(8,128)} %param.4) | copy-start | bytes 2583556
  83.7 81.9 %all-to-all-start.2 = ((f32[16,1,4608]{2,1,0:T(1,128)}), f32[16,1,4608]{2,1,0:T(1,128)S(1)}, u32[]{:S(2)}, u32[]{:S(2)}) async-start(f32[16,1,4608]{2,1,0:T(1,128)} %reshape.41), calls=%async_computation.2 | async-start | bytes 589824 | tf_op jit(solution)/shard_map/all_to_all | solution.py:250
  160.4 1.1 slice-start
  165.7 18.6 %all-to-all-start.3 = ((f32[128,1,1152]{2,1,0:T(1,128)}), f32[128,1,1152]{2,1,0:T(1,128)S(1)}, u32[]{:S(2)}, u32[]{:S(2)}) async-start(f32[128,1,1152]{2,1,0:T(1,128)} %reshape.39), calls=%async_computation.3 | async-start | bytes 1179648 | tf_op jit(solution)/shard_map/all_to_all | solution.py:254
Sparse Core Ops, SparseCore 0:
  9.5 56.2 all-gather.2

commit v4 on v0

v4 whole, which is shorter than its diff:
```python
import functools

import jax
import jax.numpy as jnp
from jax import lax
from jax.experimental import pallas as pl
from jax.experimental.pallas import tpu as pltpu
from jax.sharding import PartitionSpec as P

PRECISE = lax.Precision.HIGHEST
F32 = jnp.float32
BF16 = jnp.bfloat16
LANES = 128
NT = (((1,), (1,)), ((), ()))


def split3(x):
    hi = x.astype(BF16)
    rest = x - hi.astype(F32)
    mid = rest.astype(BF16)
    lo = (rest - mid.astype(F32)).astype(BF16)
    return hi, mid, lo


def split3_xla(x):
    hi = lax.reduce_precision(x, 8, 7)
    rest = x - hi
    mid = lax.reduce_precision(rest, 8, 7)
    return hi.astype(BF16), mid.astype(BF16), (rest - mid).astype(BF16)


def left_terms(x):
    hi, mid, lo = split3_xla(x)
    return jnp.concatenate([hi, hi, mid, hi, mid, lo], axis=-1)


def mesh_pos():
    aux = lax.axis_index('aux')
    return aux // 4, lax.rem(aux, 4), lax.axis_index('x'), lax.axis_index('core')


def peer(k):
    z, y, x, _ = mesh_pos()
    to_aux = lax.rem(z + k // 16, 4) * 4 + lax.rem(y + lax.rem(k // 4, 4), 4)
    return to_aux, lax.rem(x + lax.rem(k, 4), 4)


def push(src, dst, send_sem, recv_sem, **to):
    copy = pltpu.make_async_remote_copy(src, dst, send_sem, recv_sem, device_id=to, device_id_type=pl.DeviceIdType.MESH)
    copy.start()
    return copy


def await_bytes(like, sem):
    pltpu.make_async_copy(like, like, sem).wait()


def fock_kernel(ints_hbm, orb_ref, dens_ref, met_blk, out_ref,
                ints, wide, send, own, other, met, fit, kacc, kin, kout, kall,
                gam, gall, gsum, gpeer, gfit, gfit2, wb, jm, jt, jall,
                ints_sem, met_send, met_recv, col_send, col_recv, pair_send, pair_recv, msg_send, msg_recv):
    z, y, x, core = mesh_pos()
    aux = z * 4 + y
    n_src, cols, m_loc, _ = send.shape
    n_aux, _, n_fit = met.shape
    n_x = n_src // n_aux
    me = aux * n_x + x
    tiles, _, _, _ = ints.shape
    q_loc = ints_hbm.shape[0]
    n_col = n_src * cols
    groups = m_loc // 8
    tile = 256
    n_out = 24
    half_rows = LANES // 2

    copies = [
        [pltpu.make_async_copy(
            ints_hbm.at[:, pl.ds(8 * g, 8), pl.ds(LANES * t, LANES)],
            ints.at[t, pl.ds(0, q_loc), pl.ds(8 * g, 8), :], ints_sem.at[g, t]) for t in range(tiles)]
        for g in range(groups)]
    for group in copies:
        for copy in group:
            copy.start()
    barrier = pltpu.get_barrier_semaphore()

    def tell(k, carry):
        to_aux, to_x = peer(k)
        pl.semaphore_signal(barrier, inc=1, device_id={'aux': to_aux, 'x': to_x}, device_id_type=pl.DeviceIdType.MESH)
        return carry

    lax.fori_loop(1, n_src, tell, 0)
    pl.semaphore_signal(barrier, inc=1, device_id={'core': 1 - core}, device_id_type=pl.DeviceIdType.MESH)
    met[aux] = met_blk[:, pl.ds(pl.multiple_of(core * n_fit, n_fit), n_fit)].astype(BF16)
    ints[:, pl.ds(q_loc, LANES - q_loc)] = jnp.zeros((tiles, LANES - q_loc, m_loc, LANES), F32)
    flat = ints.reshape(tiles, LANES * m_loc, LANES)
    gam[...] = jnp.zeros_like(gam)

    upper, lower = pl.ds(0, half_rows), pl.ds(half_rows, half_rows)

    def gather_first():
        for d in range(1, 4):
            push(met.at[aux, upper], met.at[aux, upper], met_send.at[0], met_recv.at[0], aux=z * 4 + lax.rem(y + d, 4))
            push(met.at[aux, lower], met.at[aux, lower], met_send.at[1], met_recv.at[1], aux=lax.rem(z + d, 4) * 4 + y)

    def gather_second():
        three = met.at[pl.ds(0, 3), upper]
        await_bytes(three, met_recv.at[0])
        await_bytes(three, met_recv.at[1])
        for d in range(1, 4):
            for b in range(4):
                push(met.at[z * 4 + b, upper], met.at[z * 4 + b, upper], met_send.at[2], met_recv.at[2], aux=lax.rem(z + d, 4) * 4 + y)
                push(met.at[b * 4 + y, lower], met.at[b * 4 + y, lower], met_send.at[3], met_recv.at[3], aux=z * 4 + lax.rem(y + d, 4))

    for g in range(groups):
        for copy in copies[g]:
            copy.wait()

        def pair_step(j, carry, g=g):
            m = 8 * g + 2 * j
            rows = jnp.concatenate([
                jnp.concatenate([flat[t, pl.ds(m + u, LANES, stride=m_loc), :] for t in range(tiles)], axis=1)
                for u in range(2)], axis=0)
            hi, mid, lo = split3(rows)
            right = jnp.concatenate([hi, mid, hi, lo, mid, hi], axis=1)
            left = jnp.concatenate([orb_ref[...], dens_ref[4 * g + j]], axis=0)
            res = lax.dot_general(left, right, NT, preferred_element_type=F32)
            wide[pl.ds(m, n_col, stride=m_loc), :] = res[:n_col, :LANES]
            wide[pl.ds(m + 1, n_col, stride=m_loc), :] = res[:n_col, LANES:]
            gam[...] += res[n_col:n_col + 8, :LANES] + res[n_col + 8:, LANES:]
            return carry

        lax.fori_loop(0, 4, pair_step, 0)
        if g == 0:
            pl.semaphore_wait(barrier, n_src)
            gather_first()
        if g == 3:
            gather_second()

    def send_gamma(k, carry):
        to_aux, to_x = peer(k)
        push(gam, gall.at[me], msg_send.at[0], msg_recv.at[0], aux=to_aux, x=to_x)
        return carry

    lax.fori_loop(1, n_src, send_gamma, 0)
    gall[me] = gam[...]

    def send_col(c, carry):
        def narrow(k, carry):
            to_aux, to_x = peer(k)
            to = to_aux * n_x + to_x
            start = pl.multiple_of(to * (cols * m_loc) + c * m_loc, m_loc)
            send[to, c] = wide[pl.ds(start, m_loc), :].astype(BF16)
            return carry

        def send_one(k, carry):
            to_aux, to_x = peer(k)
            push(send.at[to_aux * n_x + to_x, c], own.at[c, me], col_send.at[c], col_recv.at[c], aux=to_aux, x=to_x)
            return carry

        lax.fori_loop(0, n_src, narrow, 0)
        lax.fori_loop(1, n_src, send_one, 0)
        own[c, me] = send[me, c]
        return carry

    lax.fori_loop(0, cols, send_col, 0)

    await_bytes(gall.at[pl.ds(1, n_src - 1)], msg_recv.at[0])
    for a in range(n_aux):
        gsum[a] = (gall[n_x * a] + gall[n_x * a + 1]) + (gall[n_x * a + 2] + gall[n_x * a + 3])
    push(gsum, gpeer, msg_send.at[1], msg_recv.at[1], core=1 - core).wait()
    twelve = met.at[pl.ds(0, 12), upper]
    await_bytes(twelve, met_recv.at[2])
    await_bytes(twelve, met_recv.at[3])
    tot = None
    for s in range(n_aux // 2):
        pair = jnp.concatenate([gsum[2 * s + t] + gpeer[2 * s + t] for t in range(2)], axis=1)
        hi, mid, lo = (v.astype(F32) for v in split3(pair))
        left = jnp.concatenate([hi, mid, lo, jnp.zeros_like(hi)], axis=0).astype(BF16)
        part = jnp.dot(left, met[pl.ds(2 * s, 2)].reshape(2 * LANES, n_fit), preferred_element_type=F32)
        tot = part if tot is None else tot + part
    gfit[...] = tot[0:8] + tot[8:16] + tot[16:24]
    push(gfit, gfit2, msg_send.at[2], msg_recv.at[2], core=1 - core).wait()
    low = jnp.where(core == 0, gfit[...], gfit2[...])
    high = jnp.where(core == 0, gfit2[...], gfit[...])
    wts = lax.dot_general(met_blk[...], jnp.concatenate([low, high], axis=1), NT, precision=PRECISE, preferred_element_type=F32)
    dens = wb.shape[0]
    for d in range(dens):
        wb[d] = jnp.broadcast_to(wts[:, d:d + 1], (LANES, LANES))
    jm[...] = jnp.zeros_like(jm)

    def coul_group(g, carry):
        def q_step(q, acc):
            rows = [ints[t, q, pl.ds(pl.multiple_of(8 * g, 8), 8), :] for t in range(tiles)]
            return tuple(acc[d * tiles + t] + wb[d, pl.ds(q, 1), :] * rows[t] for d in range(dens) for t in range(tiles))

        acc = lax.fori_loop(0, q_loc, q_step, tuple(jnp.zeros((8, LANES), F32) for _ in range(dens * tiles)), unroll=4)
        for d in range(dens):
            for t in range(tiles):
                jm[d // 2, pl.ds(pl.multiple_of((d % 2) * half_rows + 8 * g, 8), 8), pl.ds(LANES * t, LANES)] = acc[d * tiles + t]
        return carry

    lax.fori_loop(0, groups, coul_group, 0)
    for p in range(dens // 2):
        jt[p] = jm[p].T

    def send_coul(k, carry):
        to_aux = lax.rem(z + k // 4, 4) * 4 + lax.rem(y + lax.rem(k, 4), 4)
        push(jt.at[:, pl.ds(pl.multiple_of(to_aux * n_out, 8), n_out), :], jall.at[aux], msg_send.at[3], msg_recv.at[3], aux=to_aux)
        return carry

    lax.fori_loop(1, n_aux, send_coul, 0)
    jall[aux] = jt[:, pl.ds(pl.multiple_of(aux * n_out, 8), n_out), :]

    fit[...] = jnp.zeros_like(fit)
    kacc[...] = jnp.zeros_like(kacc)
    pad_rows = 64

    def fitted(src, c, side):
        rows = n_x * m_loc
        for n in range(n_fit // tile):
            tot = None
            for s in range(n_aux // 2):
                left = jnp.concatenate([src[c, pl.ds((2 * s + t) * n_x, n_x)].reshape(rows, LANES) for t in range(2)], axis=1)
                right = met[pl.ds(2 * s, 2), :, pl.ds(n * tile, tile)].reshape(2 * LANES, tile)
                part = jnp.dot(left, right, preferred_element_type=F32)
                tot = part if tot is None else tot + part
            for b in range(n_x):
                start = pl.multiple_of((side * n_x + b) * pad_rows, pad_rows)
                fit[pl.ds(start, m_loc), pl.ds(n * tile, tile)] = tot[b * m_loc:(b + 1) * m_loc]

    def col_step(c, carry):
        await_bytes(own.at[c, pl.ds(1, n_src - 1)], col_recv.at[c])
        swap = push(own.at[c], other.at[c], pair_send.at[c], pair_recv.at[c], core=1 - core)
        fitted(own, c, core)
        swap.wait()
        fitted(other, c, 1 - core)
        for n in range(n_fit // tile):
            hi, mid, lo = split3(fit[:, pl.ds(n * tile, tile)])
            short = [jnp.concatenate([v[pad_rows * b:pad_rows * b + m_loc] for b in range(2 * n_x)], axis=0) for v in (hi, mid, lo)]
            left = jnp.concatenate([short[0], short[0], short[1], short[0], short[1], short[2]], axis=1)
            right = jnp.concatenate([hi, mid, hi, lo, mid, hi], axis=1)
            kacc[...] += lax.dot_general(left, right, NT, preferred_element_type=F32)
        return carry

    lax.fori_loop(0, cols, col_step, 0)

    width = n_x * pad_rows
    mine = pl.multiple_of(core * width, width)
    theirs = pl.multiple_of((1 - core) * width, width)
    push(kacc.at[:, pl.ds(theirs, width)], kin, msg_send.at[4], msg_recv.at[4], core=1 - core).wait()
    ksum = kacc[:, pl.ds(mine, width)] + kin[...]
    for t in range(width // LANES):
        kout[t] = ksum[:, t * LANES:(t + 1) * LANES]

    def rows_of(to_aux):
        start = lax.rem(to_aux // 2, 2) * (n_x * m_loc) + to_aux // 4 * m_loc + lax.rem(to_aux, 2) * n_out
        return pl.ds(pl.multiple_of(start, 8), n_out)

    def send_exch(k, carry):
        to_aux, to_x = peer(k)
        push(kout.at[to_x // 2, rows_of(to_aux)], kall.at[me], msg_send.at[5], msg_recv.at[5], aux=to_aux, x=to_x)
        return carry

    lax.fori_loop(1, n_src, send_exch, 0)
    kall[me] = kout[x // 2, rows_of(aux)]
    await_bytes(jall.at[pl.ds(1, n_aux - 1)], msg_recv.at[3])
    await_bytes(kall.at[pl.ds(1, n_src - 1)], msg_recv.at[5])
    per = n_src // dens
    for d in range(dens):
        coul = jall[0, d // 2]
        for a in range(1, n_aux):
            coul = coul + jall[a, d // 2]
        coul = pltpu.roll(coul, half_rows, 1) if d % 2 else coul
        exch = kall[per * d]
        for i in range(1, per):
            exch = exch + kall[per * d + i]
        exch = jnp.where(lax.rem(x, 2) == 1, pltpu.roll(exch, half_rows, 1), exch)
        out_ref[d] = 2.0 * coul - exch

    for c in range(cols):
        await_bytes(own.at[c, pl.ds(1, n_src - 1)], col_send.at[c])
    await_bytes(gall.at[pl.ds(1, n_src - 1)], msg_send.at[0])
    await_bytes(jall.at[pl.ds(1, n_aux - 1)], msg_send.at[3])
    await_bytes(kall.at[pl.ds(1, n_src - 1)], msg_send.at[5])
    for i, n in enumerate((3, 3, 12, 12)):
        await_bytes(met.at[pl.ds(0, n), upper], met_send.at[i])


def fock_build(ints_blk, orb_terms, dens_terms, met_blk, n_aux, dens):
    q_loc, m_loc, n_bas = ints_blk.shape
    n_col = orb_terms.shape[0]
    n_x = n_bas // m_loc // 2
    chips = n_aux * n_x
    cols = n_col // chips
    n_fit = met_blk.shape[1] // 2
    n_out = n_bas // n_aux
    tiles = n_bas // LANES
    vmem = pl.BlockSpec(memory_space=pltpu.VMEM)
    dma = pltpu.SemaphoreType.DMA
    return pl.pallas_call(
        fock_kernel,
        out_shape=jax.ShapeDtypeStruct((dens, n_out, LANES), F32),
        in_specs=[pl.BlockSpec(memory_space=pl.ANY), vmem, vmem, vmem],
        out_specs=vmem,
        scratch_shapes=[
            pltpu.VMEM((tiles, LANES, m_loc, LANES), F32),
            pltpu.VMEM((n_col * m_loc, LANES), F32),
            pltpu.VMEM((chips, cols, m_loc, LANES), BF16),
            pltpu.VMEM((cols, chips, m_loc, LANES), BF16),
            pltpu.VMEM((cols, chips, m_loc, LANES), BF16),
            pltpu.VMEM((n_aux, LANES, n_fit), BF16),
            pltpu.VMEM((2 * n_x * 64, n_fit), F32),
            pltpu.VMEM((n_bas, 2 * n_x * 64), F32),
            pltpu.VMEM((n_bas, n_x * 64), F32),
            pltpu.VMEM((n_x // 2, n_bas, LANES), F32),
            pltpu.VMEM((chips, n_out, LANES), F32),
            pltpu.VMEM((8, LANES), F32),
            pltpu.VMEM((chips, 8, LANES), F32),
            pltpu.VMEM((n_aux, 8, LANES), F32),
            pltpu.VMEM((n_aux, 8, LANES), F32),
            pltpu.VMEM((8, n_fit), F32),
            pltpu.VMEM((8, n_fit), F32),
            pltpu.VMEM((dens, LANES, LANES), F32),
            pltpu.VMEM((dens // 2, LANES, n_bas), F32),
            pltpu.VMEM((dens // 2, n_bas, LANES), F32),
            pltpu.VMEM((n_aux, dens // 2, n_out, LANES), F32),
            dma((m_loc // 8, tiles)), dma((4,)), dma((4,)), dma((cols,)), dma((cols,)), dma((cols,)), dma((cols,)), dma((6,)), dma((6,)),
        ],
        compiler_params=pltpu.CompilerParams(vmem_limit_bytes=62 * 1024 * 1024, collective_id=0, has_side_effects=True),
        name='fock_build',
    )(ints_blk, orb_terms, dens_terms, met_blk)


def solution(mesh):
    n_aux, n_orb = mesh.shape['aux'], mesh.shape['orb']
    mesh4 = jax.sharding.Mesh(mesh.devices.reshape(1, n_aux, n_orb // 2, 2), ('sys', 'aux', 'x', 'core'))

    def local_fock(ints_blk, metric_blk, orbitals):
        q_loc, m_loc, n_bas = ints_blk.shape
        dens, _, n_occ = orbitals.shape
        orb = lax.axis_index('x') * 2 + lax.axis_index('core')
        met_pad = jnp.pad(metric_blk, ((0, LANES - q_loc), (0, -metric_blk.shape[1] % 512)))
        orb_rows = lax.dynamic_slice_in_dim(orbitals, orb * m_loc, m_loc, axis=1)
        dens_rows = jnp.einsum('dmi,dli->mdl', orb_rows, orbitals, precision=PRECISE, preferred_element_type=F32)
        dens_rows = jnp.pad(dens_rows, ((0, 0), (0, 8 - dens), (0, 0))).reshape(m_loc // 2, 16, n_bas)
        orb_cols = orbitals.transpose(0, 2, 1).reshape(dens * n_occ, n_bas)
        out = fock_build(ints_blk, left_terms(orb_cols), left_terms(dens_rows), met_pad, n_aux, dens)
        return out[:, :, :m_loc].transpose(0, 2, 1)

    return jax.shard_map(
        local_fock, mesh=mesh4,
        in_specs=(P(('sys', 'aux'), ('x', 'core'), None), P(('sys', 'aux'), None), P('sys', None, None)),
        out_specs=P('sys', ('x', 'core'), 'aux'), check_vma=False)
```

time: 1850 us -> 148 us (0.08)
  waiting for transfers between devices: 1200 us -> 0 us
  matrix products: 511 us -> 1.77 us
  Pallas kernels: 0 us -> 137 us
  blocking collectives: 109 us -> 0 us
    all_gather x2 -> x0, waiting for transfers between devices: 1120 us -> none  [the longest x1 959 us: local_fock(): half_all = lax.all_gather(half_tr, 'aux', axis=0, tiled=True)]
    dot_general x6 -> x1, matrix products: 511 us -> 1.77 us  [local_fock(): jnp.einsum('dmi,dli->mdl', orb_rows, orbitals, precision=PRECISE, preferr...]
    pallas_call x0 -> x1, Pallas kernels: none -> 137 us  [fock_build(): pl.pallas_call(fock_kernel, out_shape=jax.ShapeDtypeStruct((dens, n_out,...]
    unnamed x4 -> x0, waiting for transfers between devices: 85.9 us -> none
    unnamed x1 -> x0, blocking collectives: 72.1 us -> none
    all_gather x1 -> x0, blocking collectives: 23.1 us -> none  [local_fock(): gamma_all = lax.all_gather(gamma_raw, 'aux', axis=1, tiled=True)]
  transfers between devices with their start and end apart: 3 -> 0, of which waited for: 3 -> 0; matrix products, arithmetic and copies ran while one was open for 1% -> 0% of each run, Pallas kernels for 0% -> 0%
where the time goes in v4:
time: 148 us; the launch traced here: 147 us
  Pallas kernels  137 us (93%)
  local copies, waits for them, and re-layouts  7.9 us (5%)
  matrix products  1.77 us (1%)
    pallas_call x1, Pallas kernels, fock_build(): pl.pallas_call(fock_kernel, out_shape=jax.ShapeDtypeStruct((dens, n_out,...  137 us
    unnamed x12, local copies, waits for them, and re-layouts  4.55 us

profile of v4, /device:TPU:0, one launch (start us, length us, event | category | flops | bytes accessed | tf_op | source)
XLA Modules:
  0.0 147.2 jit_solution(18388170087003627063)
XLA Ops:
  0.0 1.8 %convolution_bitcast_fusion = f32[48,4,384]{2,0,1:T(8,128)S(1)} fusion(f32[4,384,80]{1,2,0:T(8,128)} %param.5, s32[]{:T(128)S(6)} %select_n.3), kind=kOutput, calls=%fused_computation | convolution fusion | flops 70778880 | bytes 950276 | tf_op jit(solution)/shard_map/dmi,dli->mdl/dot_general | solution.py:344
  1.8 0.1 copy.7
  2.0 0.1 constant_dynamic-update-slice_fusion.7
  2.1 0.0 copy-start.1
  2.1 0.1 fusion.4
  2.2 0.1 constant_dynamic-update-slice_fusion.6
  2.2 0.1 fusion.5
  2.3 0.1 fusion.2.dens_ref
  2.4 0.7 copy-done.1
  3.1 0.0 copy-start
  3.1 0.1 fusion.1
  3.2 0.0 copy-start.2
  3.2 0.7 constant_dynamic-update-slice_fusion.5
  4.0 0.8 constant_dynamic-update-slice_fusion.4
  4.8 0.7 constant_dynamic-update-slice_fusion.3
  5.5 0.7 constant_dynamic-update-slice_fusion.2
  6.2 0.8 constant_dynamic-update-slice_fusion.1
  7.0 0.0 copy-done
  7.0 0.8 constant_dynamic-update-slice_fusion.orb_ref
  7.8 0.0 copy-done.2
  7.8 1.1 pad.9.met_blk
  8.9 136.9 %fock_build.1 = f32[4,24,128]{2,1,0:T(8,128)} custom-call(f32[116,48,384]{2,1,0:T(8,128)} %ints_hbm.1, bf16[320,2304]{1,0:T(8,128)(2,1)} %constant_dynamic-update-slice_fusion.orb_ref, bf16[24,16,2304]{2,1,0:T(8,128)(2,1)} %copy-done, f32[128,2048]{1,0:T(8,128)} %pad.9.met_blk), custom_call_target="tpu_custom_call" | custom-call | tf_op jit(solution)/shard_map/fock_build/pallas_call | solution.py:300
  145.8 1.4 slice_bitcast_fusion
  (2 shorter events, 0.1 us)
Async XLA Ops:
  2.1 1.0 copy-start.1
  3.1 3.9 %copy-start = (bf16[24,16,2304]{2,1,0:T(8,128)(2,1)}, bf16[24,16,2304]{2,1,0:T(8,128)(2,1)S(1)}, u32[]{:S(2)}) copy-start(bf16[24,16,2304]{2,1,0:T(8,128)(2,1)S(1)} %fusion.2.dens_ref) | copy-start | bytes 5308420
  3.2 4.6 %copy-start.2 = (f32[116,1856]{1,0:T(8,128)S(1)}, f32[116,1856]{1,0:T(8,128)}, u32[]{:S(2)}) copy-start(f32[116,1856]{1,0:T(8,128)} %param.4) | copy-start | bytes 2583556

commit v5 on v4

v5 whole, which is shorter than its diff:
```python
import functools

import jax
import jax.numpy as jnp
from jax import lax
from jax.experimental import pallas as pl
from jax.experimental.pallas import tpu as pltpu
from jax.sharding import PartitionSpec as P

PRECISE = lax.Precision.HIGHEST
F32 = jnp.float32
BF16 = jnp.bfloat16
LANES = 128
NT = (((1,), (1,)), ((), ()))


def split3(x):
    hi = x.astype(BF16)
    rest = x - hi.astype(F32)
    mid = rest.astype(BF16)
    lo = (rest - mid.astype(F32)).astype(BF16)
    return hi, mid, lo


def mesh_pos():
    aux = lax.axis_index('aux')
    return aux // 4, lax.rem(aux, 4), lax.axis_index('x'), lax.axis_index('core')


def near():
    z, y, x, _ = mesh_pos()
    return [[lax.rem(p + d, 4) for d in range(4)] for p in (z, y, x)]


def batch(zs, ys, xs, b):
    for dy in range(4):
        for dx in range(4):
            dz = (b + dy + dx) % 4
            if dz or dy or dx:
                yield zs[dz] * 4 + ys[dy], xs[dx]


def push(src, dst, send_sem, recv_sem, **to):
    copy = pltpu.make_async_remote_copy(src, dst, send_sem, recv_sem, device_id=to, device_id_type=pl.DeviceIdType.MESH)
    copy.start()
    return copy


def await_bytes(like, sem):
    pltpu.make_async_copy(like, like, sem).wait()


def fock_kernel(ints_hbm, orb_ref, dens_ref, met_ref, out_ref,
                ints, wide, terms, met_blk, send, own, other, met, fit, kacc, kin, kout, kall,
                gam, gall, gsum, gpeer, gfit, fall, wb, jm, jt, jall,
                ints_sem, met_send, met_recv, col_send, col_recv, pair_send, pair_recv, msg_send, msg_recv):
    z, y, x, core = mesh_pos()
    zs, ys, xs = near()
    aux = z * 4 + y
    n_src, cols, m_loc, _ = send.shape
    n_aux, _, n_fit = met.shape
    n_x = n_src // n_aux
    me = aux * n_x + x
    tiles, _, m_pad, _ = ints.shape
    q_loc = ints_hbm.shape[0]
    skip = wide.shape[0] // (n_src * cols)
    n_col = n_src * cols
    groups = m_loc // 8
    tile = 256
    n_out = 24
    half_rows = LANES // 2

    copies = [
        [pltpu.make_async_copy(
            ints_hbm.at[:, pl.ds(8 * g, 8), pl.ds(LANES * t, LANES)],
            ints.at[t, pl.ds(0, q_loc), pl.ds(8 * g, 8), :], ints_sem.at[g, t]) for t in range(tiles)]
        for g in range(groups)]
    for group in copies:
        for copy in group:
            copy.start()
    barrier = pltpu.get_barrier_semaphore()

    for b in range(4):
        for to_aux, to_x in batch(zs, ys, xs, b):
            pl.semaphore_signal(barrier, inc=1, device_id={'aux': to_aux, 'x': to_x}, device_id_type=pl.DeviceIdType.MESH)
    pl.semaphore_signal(barrier, inc=1, device_id={'core': 1 - core}, device_id_type=pl.DeviceIdType.MESH)
    met_blk[...] = jnp.zeros_like(met_blk)
    for b in range(n_aux):
        met_blk[pl.ds(0, q_loc), pl.ds(b * LANES, q_loc)] = met_ref[:, b * q_loc:(b + 1) * q_loc]
    met[aux] = met_blk[:, pl.ds(pl.multiple_of(core * n_fit, n_fit), n_fit)].astype(BF16)
    ints[:, pl.ds(q_loc, LANES - q_loc)] = jnp.zeros((tiles, LANES - q_loc, m_pad, LANES), F32)
    flat = ints.reshape(tiles, LANES * m_pad, LANES)
    for i, term in enumerate(split3(orb_ref[...])):
        terms[i] = term
    gam[...] = jnp.zeros_like(gam)

    upper, lower = pl.ds(0, half_rows), pl.ds(half_rows, half_rows)

    def gather_first():
        for d in range(1, 4):
            push(met.at[aux, upper], met.at[aux, upper], met_send.at[0], met_recv.at[0], aux=z * 4 + ys[d])
            push(met.at[aux, lower], met.at[aux, lower], met_send.at[1], met_recv.at[1], aux=zs[d] * 4 + y)

    def gather_second():
        three = met.at[pl.ds(0, 3), upper]
        await_bytes(three, met_recv.at[0])
        await_bytes(three, met_recv.at[1])
        for d in range(1, 4):
            for b in range(4):
                push(met.at[z * 4 + b, upper], met.at[z * 4 + b, upper], met_send.at[2], met_recv.at[2], aux=zs[d] * 4 + y)
                push(met.at[b * 4 + y, lower], met.at[b * 4 + y, lower], met_send.at[3], met_recv.at[3], aux=z * 4 + ys[d])

    for g in range(groups):
        for copy in copies[g]:
            copy.wait()

        def pair_step(j, carry, g=g):
            m = 8 * g + 2 * j
            rows = jnp.concatenate([
                jnp.concatenate([flat[t, pl.ds(m + u, LANES, stride=m_pad), :] for t in range(tiles)], axis=1)
                for u in range(2)], axis=0)
            hi, mid, lo = split3(rows)
            right = jnp.concatenate([hi, mid, hi, lo, mid, hi], axis=1)
            both = [jnp.concatenate([terms[i], v], axis=0) for i, v in enumerate(split3(dens_ref[4 * g + j]))]
            left = jnp.concatenate([both[0], both[0], both[1], both[0], both[1], both[2]], axis=1)
            res = lax.dot_general(left, right, NT, preferred_element_type=F32)
            wide[pl.ds(m, n_col, stride=skip), :] = res[:n_col, :LANES]
            wide[pl.ds(m + 1, n_col, stride=skip), :] = res[:n_col, LANES:]
            gam[...] += res[n_col:n_col + 8, :LANES] + res[n_col + 8:, LANES:]
            return carry

        lax.fori_loop(0, 4, pair_step, 0)
        if g == 0:
            pl.semaphore_wait(barrier, n_src)
            gather_first()
        if g == 3:
            gather_second()

    def narrow(c):
        def one(to, carry):
            send[to, c] = wide[pl.ds((to * cols + c) * skip, m_loc), :].astype(BF16)
            return carry

        lax.fori_loop(0, n_src, one, 0, unroll=4)

    def send_batch(c, b):
        for to_aux, to_x in batch(zs, ys, xs, b):
            push(send.at[to_aux * n_x + to_x, c], own.at[c, me], col_send.at[c], col_recv.at[c], aux=to_aux, x=to_x)

    narrow(0)
    for b in range(4):
        for to_aux, to_x in batch(zs, ys, xs, b):
            push(gam, gall.at[me], msg_send.at[0], msg_recv.at[0], aux=to_aux, x=to_x)
    gall[me] = gam[...]
    for b in range(4):
        send_batch(0, b)
    for c in range(1, cols):
        narrow(c)
    for c in range(cols):
        own[c, me] = send[me, c]

    await_bytes(gall.at[pl.ds(1, n_src - 1)], msg_recv.at[0])
    for a in range(n_aux):
        gsum[a] = (gall[n_x * a] + gall[n_x * a + 1]) + (gall[n_x * a + 2] + gall[n_x * a + 3])
    swap = push(gsum, gpeer, msg_send.at[1], msg_recv.at[1], core=1 - core)
    send_batch(1, 0)
    send_batch(1, 1)
    swap.wait()

    def times_met(blocks):
        return lax.dot_general(jnp.concatenate(blocks, axis=1), met_blk[...], NT, precision=PRECISE, preferred_element_type=F32)

    gfit[...] = times_met([gsum[a] + gpeer[a] for a in range(n_aux)])
    for dz in range(4):
        for dy in range(4):
            if dz or dy:
                push(gfit, fall.at[aux], msg_send.at[2], msg_recv.at[2], aux=zs[dz] * 4 + ys[dy])
    fall[aux] = gfit[...]
    send_batch(1, 2)
    send_batch(1, 3)
    await_bytes(fall.at[pl.ds(1, n_aux - 1)], msg_recv.at[2])
    wts = lax.dot_general(met_blk[...], jnp.concatenate([fall[a] for a in range(n_aux)], axis=1), NT, precision=PRECISE, preferred_element_type=F32)
    dens = wb.shape[0]
    for d in range(dens):
        wb[d] = jnp.broadcast_to(wts[:, d:d + 1], (LANES, LANES))
    jm[...] = jnp.zeros_like(jm)

    def coul_group(g, carry):
        def q_step(q, acc):
            rows = [ints[t, q, pl.ds(pl.multiple_of(8 * g, 8), 8), :] for t in range(tiles)]
            return tuple(acc[d * tiles + t] + wb[d, pl.ds(q, 1), :] * rows[t] for d in range(dens) for t in range(tiles))

        acc = lax.fori_loop(0, q_loc, q_step, tuple(jnp.zeros((8, LANES), F32) for _ in range(dens * tiles)), unroll=4)
        for d in range(dens):
            for t in range(tiles):
                jm[d // 2, pl.ds(pl.multiple_of((d % 2) * half_rows + 8 * g, 8), 8), pl.ds(LANES * t, LANES)] = acc[d * tiles + t]
        return carry

    for b in range(2):
        lax.fori_loop(b * groups // 2, (b + 1) * groups // 2, coul_group, 0)
        send_batch(2, 2 * b)
        send_batch(2, 2 * b + 1)
    for p in range(dens // 2):
        jt[p] = jm[p].T

    for dz in range(4):
        for dy in range(4):
            if dz or dy:
                to_aux = zs[dz] * 4 + ys[dy]
                push(jt.at[:, pl.ds(pl.multiple_of(to_aux * n_out, 8), n_out), :], jall.at[aux], msg_send.at[3], msg_recv.at[3], aux=to_aux)
    jall[aux] = jt[:, pl.ds(pl.multiple_of(aux * n_out, 8), n_out), :]

    fit[...] = jnp.zeros_like(fit)
    kacc[...] = jnp.zeros_like(kacc)
    pad_rows = 64

    def fitted(src, c, side):
        rows = n_x * m_loc
        for n in range(n_fit // tile):
            tot = None
            for s in range(n_aux // 2):
                left = jnp.concatenate([src[c, pl.ds((2 * s + t) * n_x, n_x)].reshape(rows, LANES) for t in range(2)], axis=1)
                right = met[pl.ds(2 * s, 2), :, pl.ds(n * tile, tile)].reshape(2 * LANES, tile)
                part = jnp.dot(left, right, preferred_element_type=F32)
                tot = part if tot is None else tot + part
            for b in range(n_x):
                start = pl.multiple_of((side * n_x + b) * pad_rows, pad_rows)
                fit[pl.ds(start, m_loc), pl.ds(n * tile, tile)] = tot[b * m_loc:(b + 1) * m_loc]

    twelve = met.at[pl.ds(0, 12), upper]
    await_bytes(twelve, met_recv.at[2])
    await_bytes(twelve, met_recv.at[3])

    def col_step(c, carry):
        def more(b):
            @pl.when(c < cols - 3)
            def _():
                send_batch(c + 3, b)

        more(0)
        await_bytes(own.at[c, pl.ds(1, n_src - 1)], col_recv.at[c])
        swap = push(own.at[c], other.at[c], pair_send.at[c], pair_recv.at[c], core=1 - core)
        fitted(own, c, core)
        more(1)
        swap.wait()
        fitted(other, c, 1 - core)
        more(2)
        for n in range(n_fit // tile):
            hi, mid, lo = split3(fit[:, pl.ds(n * tile, tile)])
            short = [jnp.concatenate([v[pad_rows * b:pad_rows * b + m_loc] for b in range(2 * n_x)], axis=0) for v in (hi, mid, lo)]
            left = jnp.concatenate([short[0], short[0], short[1], short[0], short[1], short[2]], axis=1)
            right = jnp.concatenate([hi, mid, hi, lo, mid, hi], axis=1)
            kacc[...] += lax.dot_general(left, right, NT, preferred_element_type=F32)
            if n == 1:
                more(3)
        return carry

    lax.fori_loop(0, cols, col_step, 0)

    width = n_x * pad_rows
    mine = pl.multiple_of(core * width, width)
    theirs = pl.multiple_of((1 - core) * width, width)
    push(kacc.at[:, pl.ds(theirs, width)], kin, msg_send.at[4], msg_recv.at[4], core=1 - core).wait()
    ksum = kacc[:, pl.ds(mine, width)] + kin[...]
    for t in range(width // LANES):
        kout[t] = ksum[:, t * LANES:(t + 1) * LANES]

    def rows_of(to_aux):
        start = lax.rem(to_aux // 2, 2) * (n_x * m_loc) + to_aux // 4 * m_loc + lax.rem(to_aux, 2) * n_out
        return pl.ds(pl.multiple_of(start, 8), n_out)

    for b in range(4):
        for to_aux, to_x in batch(zs, ys, xs, b):
            push(kout.at[to_x // 2, rows_of(to_aux)], kall.at[me], msg_send.at[5], msg_recv.at[5], aux=to_aux, x=to_x)
    kall[me] = kout[x // 2, rows_of(aux)]
    await_bytes(jall.at[pl.ds(1, n_aux - 1)], msg_recv.at[3])
    await_bytes(kall.at[pl.ds(1, n_src - 1)], msg_recv.at[5])
    per = n_src // dens
    for d in range(dens):
        coul = jall[0, d // 2]
        for a in range(1, n_aux):
            coul = coul + jall[a, d // 2]
        coul = pltpu.roll(coul, half_rows, 1) if d % 2 else coul
        exch = kall[per * d]
        for i in range(1, per):
            exch = exch + kall[per * d + i]
        exch = jnp.where(lax.rem(x, 2) == 1, pltpu.roll(exch, half_rows, 1), exch)
        out_ref[d] = 2.0 * coul - exch

    for c in range(cols):
        await_bytes(own.at[c, pl.ds(1, n_src - 1)], col_send.at[c])
    await_bytes(gall.at[pl.ds(1, n_src - 1)], msg_send.at[0])
    await_bytes(fall.at[pl.ds(1, n_aux - 1)], msg_send.at[2])
    await_bytes(jall.at[pl.ds(1, n_aux - 1)], msg_send.at[3])
    await_bytes(kall.at[pl.ds(1, n_src - 1)], msg_send.at[5])
    for i, n in enumerate((3, 3, 12, 12)):
        await_bytes(met.at[pl.ds(0, n), upper], met_send.at[i])


def fock_build(ints_blk, orb_cols, dens_rows, metric_blk, n_aux, dens):
    q_loc, m_loc, n_bas = ints_blk.shape
    n_col = orb_cols.shape[0]
    n_x = n_bas // m_loc // 2
    chips = n_aux * n_x
    cols = n_col // chips
    n_fit = n_aux // 2 * LANES
    n_out = n_bas // n_aux
    tiles = n_bas // LANES
    vmem = pl.BlockSpec(memory_space=pltpu.VMEM)
    dma = pltpu.SemaphoreType.DMA
    return pl.pallas_call(
        fock_kernel,
        out_shape=jax.ShapeDtypeStruct((dens, n_out, LANES), F32),
        in_specs=[pl.BlockSpec(memory_space=pl.ANY), vmem, vmem, vmem],
        out_specs=vmem,
        scratch_shapes=[
            pltpu.VMEM((tiles, LANES, m_loc + 8, LANES), F32),
            pltpu.VMEM((n_col * (m_loc + 1), LANES), F32),
            pltpu.VMEM((3, n_col, n_bas), BF16),
            pltpu.VMEM((LANES, 2 * n_fit), F32),
            pltpu.VMEM((chips, cols, m_loc, LANES), BF16),
            pltpu.VMEM((cols, chips, m_loc, LANES), BF16),
            pltpu.VMEM((cols, chips, m_loc, LANES), BF16),
            pltpu.VMEM((n_aux, LANES, n_fit), BF16),
            pltpu.VMEM((2 * n_x * 64, n_fit), F32),
            pltpu.VMEM((n_bas, 2 * n_x * 64), F32),
            pltpu.VMEM((n_bas, n_x * 64), F32),
            pltpu.VMEM((n_x // 2, n_bas, LANES), F32),
            pltpu.VMEM((chips, n_out, LANES), F32),
            pltpu.VMEM((8, LANES), F32),
            pltpu.VMEM((chips, 8, LANES), F32),
            pltpu.VMEM((n_aux, 8, LANES), F32),
            pltpu.VMEM((n_aux, 8, LANES), F32),
            pltpu.VMEM((8, LANES), F32),
            pltpu.VMEM((n_aux, 8, LANES), F32),
            pltpu.VMEM((dens, LANES, LANES), F32),
            pltpu.VMEM((dens // 2, LANES, n_bas), F32),
            pltpu.VMEM((dens // 2, n_bas, LANES), F32),
            pltpu.VMEM((n_aux, dens // 2, n_out, LANES), F32),
            dma((m_loc // 8, tiles)), dma((4,)), dma((4,)), dma((cols,)), dma((cols,)), dma((cols,)), dma((cols,)), dma((6,)), dma((6,)),
        ],
        compiler_params=pltpu.CompilerParams(vmem_limit_bytes=62 * 1024 * 1024, collective_id=0, has_side_effects=True),
        name='fock_build',
    )(ints_blk, orb_cols, dens_rows, metric_blk)


def solution(mesh):
    n_aux, n_orb = mesh.shape['aux'], mesh.shape['orb']
    mesh4 = jax.sharding.Mesh(mesh.devices.reshape(1, n_aux, n_orb // 2, 2), ('sys', 'aux', 'x', 'core'))

    def local_fock(ints_blk, metric_blk, orbitals):
        q_loc, m_loc, n_bas = ints_blk.shape
        dens, _, n_occ = orbitals.shape
        orb = lax.axis_index('x') * 2 + lax.axis_index('core')
        orb_rows = lax.dynamic_slice_in_dim(orbitals, orb * m_loc, m_loc, axis=1)
        dens_rows = jnp.einsum('dmi,dli->mdl', orb_rows, orbitals, precision=PRECISE, preferred_element_type=F32)
        dens_rows = jnp.pad(dens_rows, ((0, 0), (0, 8 - dens), (0, 0))).reshape(m_loc // 2, 16, n_bas)
        orb_cols = orbitals.transpose(0, 2, 1).reshape(dens * n_occ, n_bas)
        out = fock_build(ints_blk, orb_cols, dens_rows, metric_blk, n_aux, dens)
        return out[:, :, :m_loc].transpose(0, 2, 1)

    return jax.shard_map(
        local_fock, mesh=mesh4,
        in_specs=(P(('sys', 'aux'), ('x', 'core'), None), P(('sys', 'aux'), None), P('sys', None, None)),
        out_specs=P('sys', ('x', 'core'), 'aux'), check_vma=False)
```

time: 148 us -> 131 us (0.89)
  Pallas kernels: 137 us -> 127 us
  local copies, waits for them, and re-layouts: 7.9 us -> 2.39 us
    pallas_call x1, Pallas kernels: 137 us -> 127 us  [fock_build(): pl.pallas_call(fock_kernel, out_shape=jax.ShapeDtypeStruct((dens, n_out,...]
    unnamed x12 -> x1, local copies, waits for them, and re-layouts: 4.55 us -> 0.12 us
where the time goes in v5:
time: 131 us
  Pallas kernels  127 us (97%)
  local copies, waits for them, and re-layouts  2.39 us (2%)
  matrix products  1.7 us (1%)
    pallas_call x1, Pallas kernels, fock_build(): pl.pallas_call(fock_kernel, out_shape=jax.ShapeDtypeStruct((dens, n_out,...  127 us

profile of v5, /device:TPU:0, one launch (start us, length us, event | category | flops | bytes accessed | tf_op | source)
XLA Modules:
  0.0 130.9 jit_solution(5481958793567706841)
XLA Ops:
  0.0 1.7 %convolution_bitcast_fusion = f32[48,4,384]{2,0,1:T(8,128)S(1)} fusion(f32[4,384,80]{1,2,0:T(8,128)} %param.5, s32[]{:T(128)S(6)} %select_n.3), kind=kOutput, calls=%fused_computation | convolution fusion | flops 70778880 | bytes 950276 | tf_op jit(solution)/shard_map/dmi,dli->mdl/dot_general | solution.py:356
  1.7 0.1 copy.7
  1.8 0.8 pad.4.clone
  2.7 126.8 %fock_build.1 = f32[4,24,128]{2,1,0:T(8,128)} custom-call(f32[116,48,384]{2,1,0:T(8,128)} %ints_hbm.1, f32[320,384]{1,0:T(8,128)} %bitcast.10, f32[24,16,384]{2,1,0:T(8,128)} %bitcast.9, f32[116,1856]{1,0:T(8,128)} %met_ref.1), custom_call_target="tpu_custom_call" | custom-call | tf_op jit(solution)/shard_map/fock_build/pallas_call | solution.py:311
  129.5 1.4 %slice_bitcast_fusion = f32[4,48,24]{1,2,0:T(8,128)} fusion(f32[4,24,128]{2,1,0:T(8,128)} %fock_build.1), kind=kLoop, calls=%fused_computation.2 | loop fusion | bytes 36864 | tf_op jit(solution)/shard_map/transpose | solution.py:360

commit v6 on v5

--- a/solution.py
+++ b/solution.py
@@ -50,8 +50,8 @@
     pltpu.make_async_copy(like, like, sem).wait()
 
 
-def fock_kernel(ints_hbm, orb_ref, dens_ref, met_ref, out_ref,
-                ints, wide, terms, met_blk, send, own, other, met, fit, kacc, kin, kout, kall,
+def fock_kernel(ints_hbm, orb_ref, met_ref, out_ref,
+                ints, wide, terms, drows, met_blk, send, own, other, met, fit, kacc, kin, kpk, kall,
                 gam, gall, gsum, gpeer, gfit, fall, wb, jm, jt, jall,
                 ints_sem, met_send, met_recv, col_send, col_recv, pair_send, pair_recv, msg_send, msg_recv):
     z, y, x, core = mesh_pos()
@@ -90,26 +90,44 @@
     met[aux] = met_blk[:, pl.ds(pl.multiple_of(core * n_fit, n_fit), n_fit)].astype(BF16)
     ints[:, pl.ds(q_loc, LANES - q_loc)] = jnp.zeros((tiles, LANES - q_loc, m_pad, LANES), F32)
     flat = ints.reshape(tiles, LANES * m_pad, LANES)
-    for i, term in enumerate(split3(orb_ref[...])):
-        terms[i] = term
+    dens, _, n_occ = orb_ref.shape
+    drows[...] = jnp.zeros_like(drows)
+    for d in range(dens):
+        for i, term in enumerate(split3(orb_ref[d].T)):
+            terms[i, pl.ds(d * n_occ, n_occ), :] = term
+        here = orb_ref[d, pl.ds(pl.multiple_of((x * 2 + core) * m_loc, m_loc), m_loc), :]
+        full = lax.dot_general(here, orb_ref[d], NT, precision=PRECISE, preferred_element_type=F32)
+        for t in range(tiles):
+            drows[t, pl.ds(d, m_loc, stride=8), :] = full[:, t * LANES:(t + 1) * LANES]
     gam[...] = jnp.zeros_like(gam)
 
     upper, lower = pl.ds(0, half_rows), pl.ds(half_rows, half_rows)
 
+    def to_y(d, blk, half, n):
+        push(met.at[blk, half], met.at[blk, half], met_send.at[n], met_recv.at[n], aux=z * 4 + ys[d])
+
+    def to_z(d, blk, half, n):
+        push(met.at[blk, half], met.at[blk, half], met_send.at[n], met_recv.at[n], aux=zs[d] * 4 + y)
+
     def gather_first():
-        for d in range(1, 4):
-            push(met.at[aux, upper], met.at[aux, upper], met_send.at[0], met_recv.at[0], aux=z * 4 + ys[d])
-            push(met.at[aux, lower], met.at[aux, lower], met_send.at[1], met_recv.at[1], aux=zs[d] * 4 + y)
+        for d in (1, 3, 2):
+            to_y(d, aux, upper, 0)
+            to_z(d, aux, lower, 1)
+        for d in (1, 3, 2):
+            to_z(d, aux, upper, 2)
+            to_y(d, aux, lower, 3)
 
     def gather_second():
         three = met.at[pl.ds(0, 3), upper]
         await_bytes(three, met_recv.at[0])
         await_bytes(three, met_recv.at[1])
-        for d in range(1, 4):
-            for b in range(4):
-                push(met.at[z * 4 + b, upper], met.at[z * 4 + b, upper], met_send.at[2], met_recv.at[2], aux=zs[d] * 4 + y)
-                push(met.at[b * 4 + y, lower], met.at[b * 4 + y, lower], met_send.at[3], met_recv.at[3], aux=z * 4 + ys[d])
-
+        for b in range(1, 4):
+            for d in (1, 3, 2):
+                to_z(d, z * 4 + ys[b], upper, 2)
+                to_y(d, zs[b] * 4 + y, lower, 3)
+
+    pl.semaphore_wait(barrier, n_src)
+    gather_first()
     for g in range(groups):
         for copy in copies[g]:
             copy.wait()
@@ -121,7 +139,9 @@
                 for u in range(2)], axis=0)
             hi, mid, lo = split3(rows)
             right = jnp.concatenate([hi, mid, hi, lo, mid, hi], axis=1)
-            both = [jnp.concatenate([terms[i], v], axis=0) for i, v in enumerate(split3(dens_ref[4 * g + j]))]
+            at = pl.ds(pl.multiple_of(16 * (4 * g + j), 16), 16)
+            drow = jnp.concatenate([drows[t, at, :] for t in range(tiles)], axis=1)
+            both = [jnp.concatenate([terms[i], v], axis=0) for i, v in enumerate(split3(drow))]
             left = jnp.concatenate([both[0], both[0], both[1], both[0], both[1], both[2]], axis=1)
             res = lax.dot_general(left, right, NT, preferred_element_type=F32)
             wide[pl.ds(m, n_col, stride=skip), :] = res[:n_col, :LANES]
@@ -130,10 +150,7 @@
             return carry
 
         lax.fori_loop(0, 4, pair_step, 0)
-        if g == 0:
-            pl.semaphore_wait(barrier, n_src)
-            gather_first()
-        if g == 3:
+        if g == 2:
             gather_second()
 
     def narrow(c):
@@ -159,13 +176,13 @@
     for c in range(cols):
         own[c, me] = send[me, c]
 
+    for b in range(4):
+        send_batch(1, b)
+
     await_bytes(gall.at[pl.ds(1, n_src - 1)], msg_recv.at[0])
     for a in range(n_aux):
         gsum[a] = (gall[n_x * a] + gall[n_x * a + 1]) + (gall[n_x * a + 2] + gall[n_x * a + 3])
-    swap = push(gsum, gpeer, msg_send.at[1], msg_recv.at[1], core=1 - core)
-    send_batch(1, 0)
-    send_batch(1, 1)
-    swap.wait()
+    push(gsum, gpeer, msg_send.at[1], msg_recv.at[1], core=1 - core).wait()
 
     def times_met(blocks):
         return lax.dot_general(jnp.concatenate(blocks, axis=1), met_blk[...], NT, precision=PRECISE, preferred_element_type=F32)
@@ -176,39 +193,6 @@
             if dz or dy:
                 push(gfit, fall.at[aux], msg_send.at[2], msg_recv.at[2], aux=zs[dz] * 4 + ys[dy])
     fall[aux] = gfit[...]
-    send_batch(1, 2)
-    send_batch(1, 3)
-    await_bytes(fall.at[pl.ds(1, n_aux - 1)], msg_recv.at[2])
-    wts = lax.dot_general(met_blk[...], jnp.concatenate([fall[a] for a in range(n_aux)], axis=1), NT, precision=PRECISE, preferred_element_type=F32)
-    dens = wb.shape[0]
-    for d in range(dens):
-        wb[d] = jnp.broadcast_to(wts[:, d:d + 1], (LANES, LANES))
-    jm[...] = jnp.zeros_like(jm)
-
-    def coul_group(g, carry):
-        def q_step(q, acc):
-            rows = [ints[t, q, pl.ds(pl.multiple_of(8 * g, 8), 8), :] for t in range(tiles)]
-            return tuple(acc[d * tiles + t] + wb[d, pl.ds(q, 1), :] * rows[t] for d in range(dens) for t in range(tiles))
-
-        acc = lax.fori_loop(0, q_loc, q_step, tuple(jnp.zeros((8, LANES), F32) for _ in range(dens * tiles)), unroll=4)
-        for d in range(dens):
-            for t in range(tiles):
-                jm[d // 2, pl.ds(pl.multiple_of((d % 2) * half_rows + 8 * g, 8), 8), pl.ds(LANES * t, LANES)] = acc[d * tiles + t]
-        return carry
-
-    for b in range(2):
-        lax.fori_loop(b * groups // 2, (b + 1) * groups // 2, coul_group, 0)
-        send_batch(2, 2 * b)
-        send_batch(2, 2 * b + 1)
-    for p in range(dens // 2):
-        jt[p] = jm[p].T
-
-    for dz in range(4):
-        for dy in range(4):
-            if dz or dy:
-                to_aux = zs[dz] * 4 + ys[dy]
-                push(jt.at[:, pl.ds(pl.multiple_of(to_aux * n_out, 8), n_out), :], jall.at[aux], msg_send.at[3], msg_recv.at[3], aux=to_aux)
-    jall[aux] = jt[:, pl.ds(pl.multiple_of(aux * n_out, 8), n_out), :]
 
     fit[...] = jnp.zeros_like(fit)
     kacc[...] = jnp.zeros_like(kacc)
@@ -231,11 +215,10 @@
     await_bytes(twelve, met_recv.at[2])
     await_bytes(twelve, met_recv.at[3])
 
-    def col_step(c, carry):
+    def col_step(c, carry, pump=False):
         def more(b):
-            @pl.when(c < cols - 3)
-            def _():
-                send_batch(c + 3, b)
+            if pump:
+                send_batch(c + 2, b)
 
         more(0)
         await_bytes(own.at[c, pl.ds(1, n_src - 1)], col_recv.at[c])
@@ -255,24 +238,61 @@
                 more(3)
         return carry
 
-    lax.fori_loop(0, cols, col_step, 0)
+    lax.fori_loop(0, cols - 2, functools.partial(col_step, pump=True), 0)
+
+    await_bytes(fall.at[pl.ds(1, n_aux - 1)], msg_recv.at[2])
+    wts = lax.dot_general(met_blk[...], jnp.concatenate([fall[a] for a in range(n_aux)], axis=1), NT, precision=PRECISE, preferred_element_type=F32)
+    for d in range(dens):
+        wb[d] = jnp.broadcast_to(wts[:, d:d + 1], (LANES, LANES))
+    jm[...] = jnp.zeros_like(jm)
+
+    def coul_group(g, carry):
+        def q_step(q, acc):
+            rows = [ints[t, q, pl.ds(pl.multiple_of(8 * g, 8), 8), :] for t in range(tiles)]
+            return tuple(acc[d * tiles + t] + wb[d, pl.ds(q, 1), :] * rows[t] for d in range(dens) for t in range(tiles))
+
+        acc = lax.fori_loop(0, q_loc, q_step, tuple(jnp.zeros((8, LANES), F32) for _ in range(dens * tiles)), unroll=4)
+        for d in range(dens):
+            for t in range(tiles):
+                jm[d // 2, pl.ds(pl.multiple_of((d % 2) * half_rows + 8 * g, 8), 8), pl.ds(LANES * t, LANES)] = acc[d * tiles + t]
+        return carry
+
+    lax.fori_loop(0, groups, coul_group, 0)
+    for p in range(dens // 2):
+        jt[p] = jm[p].T
+
+    for dz in range(4):
+        for dy in range(4):
+            if dz or dy:
+                to_aux = zs[dz] * 4 + ys[dy]
+                push(jt.at[:, pl.ds(pl.multiple_of(to_aux * n_out, 8), n_out), :], jall.at[aux], msg_send.at[3], msg_recv.at[3], aux=to_aux)
+    jall[aux] = jt[:, pl.ds(pl.multiple_of(aux * n_out, 8), n_out), :]
+
+    lax.fori_loop(cols - 2, cols, col_step, 0)
 
     width = n_x * pad_rows
     mine = pl.multiple_of(core * width, width)
     theirs = pl.multiple_of((1 - core) * width, width)
     push(kacc.at[:, pl.ds(theirs, width)], kin, msg_send.at[4], msg_recv.at[4], core=1 - core).wait()
-    ksum = kacc[:, pl.ds(mine, width)] + kin[...]
-    for t in range(width // LANES):
-        kout[t] = ksum[:, t * LANES:(t + 1) * LANES]
-
-    def rows_of(to_aux):
-        start = lax.rem(to_aux // 2, 2) * (n_x * m_loc) + to_aux // 4 * m_loc + lax.rem(to_aux, 2) * n_out
-        return pl.ds(pl.multiple_of(start, 8), n_out)
+    left_side = lax.broadcasted_iota(jnp.int32, (8, LANES), 1) < pad_rows
+    for a in range(n_aux):
+        start = a // 2 % 2 * (n_x * m_loc) + a // 4 * m_loc + a % 2 * n_out
+        for t in range(width // LANES):
+            rows = [kacc[pl.ds(start + 8 * i, 8), pl.ds(pl.multiple_of(mine + t * LANES, LANES), LANES)]
+                    + kin[pl.ds(start + 8 * i, 8), pl.ds(t * LANES, LANES)] for i in range(3)]
+            turned = [pltpu.roll(v, pad_rows, 1) for v in rows]
+            kpk[2 * t, pl.ds(16 * a, 8)] = jnp.where(left_side, rows[0], turned[1])
+            kpk[2 * t, pl.ds(16 * a + 8, 8)] = rows[2]
+            kpk[2 * t + 1, pl.ds(16 * a, 8)] = jnp.where(left_side, turned[0], rows[1])
+            kpk[2 * t + 1, pl.ds(16 * a + 8, 8)] = turned[2]
+
+    def block_for(to_aux, to_x):
+        return kpk.at[to_x, pl.ds(pl.multiple_of(to_aux * 16, 16), 16)]
 
     for b in range(4):
         for to_aux, to_x in batch(zs, ys, xs, b):
-            push(kout.at[to_x // 2, rows_of(to_aux)], kall.at[me], msg_send.at[5], msg_recv.at[5], aux=to_aux, x=to_x)
-    kall[me] = kout[x // 2, rows_of(aux)]
+            push(block_for(to_aux, to_x), kall.at[me], msg_send.at[5], msg_recv.at[5], aux=to_aux, x=to_x)
+    kall[me] = kpk[x, pl.ds(pl.multiple_of(aux * 16, 16), 16)]
     await_bytes(jall.at[pl.ds(1, n_aux - 1)], msg_recv.at[3])
     await_bytes(kall.at[pl.ds(1, n_src - 1)], msg_recv.at[5])
     per = n_src // dens
@@ -284,7 +304,7 @@
         exch = kall[per * d]
         for i in range(1, per):
             exch = exch + kall[per * d + i]
-        exch = jnp.where(lax.rem(x, 2) == 1, pltpu.roll(exch, half_rows, 1), exch)
+        exch = jnp.concatenate([exch[:8], pltpu.roll(exch[:8], pad_rows, 1), exch[8:]], axis=0)
         out_ref[d] = 2.0 * coul - exch
 
     for c in range(cols):
@@ -297,9 +317,10 @@
         await_bytes(met.at[pl.ds(0, n), upper], met_send.at[i])
 
 
-def fock_build(ints_blk, orb_cols, dens_rows, metric_blk, n_aux, dens):
+def fock_build(ints_blk, orbitals, metric_blk, n_aux):
     q_loc, m_loc, n_bas = ints_blk.shape
-    n_col = orb_cols.shape[0]
+    dens, _, n_occ = orbitals.shape
+    n_col = dens * n_occ
     n_x = n_bas // m_loc // 2
     chips = n_aux * n_x
     cols = n_col // chips
@@ -311,12 +332,13 @@
     return pl.pallas_call(
         fock_kernel,
         out_shape=jax.ShapeDtypeStruct((dens, n_out, LANES), F32),
-        in_specs=[pl.BlockSpec(memory_space=pl.ANY), vmem, vmem, vmem],
+        in_specs=[pl.BlockSpec(memory_space=pl.ANY), vmem, vmem],
         out_specs=vmem,
         scratch_shapes=[
             pltpu.VMEM((tiles, LANES, m_loc + 8, LANES), F32),
             pltpu.VMEM((n_col * (m_loc + 1), LANES), F32),
             pltpu.VMEM((3, n_col, n_bas), BF16),
+            pltpu.VMEM((tiles, 8 * m_loc, LANES), F32),
             pltpu.VMEM((LANES, 2 * n_fit), F32),
             pltpu.VMEM((chips, cols, m_loc, LANES), BF16),
             pltpu.VMEM((cols, chips, m_loc, LANES), BF16),
@@ -325,8 +347,8 @@
             pltpu.VMEM((2 * n_x * 64, n_fit), F32),
             pltpu.VMEM((n_bas, 2 * n_x * 64), F32),
             pltpu.VMEM((n_bas, n_x * 64), F32),
-            pltpu.VMEM((n_x // 2, n_bas, LANES), F32),
-            pltpu.VMEM((chips, n_out, LANES), F32),
+            pltpu.VMEM((n_x, 16 * n_aux, LANES), F32),
+            pltpu.VMEM((chips, 16, LANES), F32),
             pltpu.VMEM((8, LANES), F32),
             pltpu.VMEM((chips, 8, LANES), F32),
             pltpu.VMEM((n_aux, 8, LANES), F32),
@@ -341,7 +363,7 @@
         ],
         compiler_params=pltpu.CompilerParams(vmem_limit_bytes=62 * 1024 * 1024, collective_id=0, has_side_effects=True),
         name='fock_build',
-    )(ints_blk, orb_cols, dens_rows, metric_blk)
+    )(ints_blk, orbitals, metric_blk)
 
 
 def solution(mesh):
@@ -349,14 +371,8 @@
     mesh4 = jax.sharding.Mesh(mesh.devices.reshape(1, n_aux, n_orb // 2, 2), ('sys', 'aux', 'x', 'core'))
 
     def local_fock(ints_blk, metric_blk, orbitals):
-        q_loc, m_loc, n_bas = ints_blk.shape
-        dens, _, n_occ = orbitals.shape
-        orb = lax.axis_index('x') * 2 + lax.axis_index('core')
-        orb_rows = lax.dynamic_slice_in_dim(orbitals, orb * m_loc, m_loc, axis=1)
-        dens_rows = jnp.einsum('dmi,dli->mdl', orb_rows, orbitals, precision=PRECISE, preferred_element_type=F32)
-        dens_rows = jnp.pad(dens_rows, ((0, 0), (0, 8 - dens), (0, 0))).reshape(m_loc // 2, 16, n_bas)
-        orb_cols = orbitals.transpose(0, 2, 1).reshape(dens * n_occ, n_bas)
-        out = fock_build(ints_blk, orb_cols, dens_rows, metric_blk, n_aux, dens)
+        m_loc = ints_blk.shape[1]
+        out = fock_build(ints_blk, orbitals, metric_blk, n_aux)
         return out[:, :, :m_loc].transpose(0, 2, 1)
 
     return jax.shard_map(

time: 131 us -> 122 us (0.931)
  Pallas kernels: 127 us -> 118 us
  matrix products: 1.7 us -> 0 us
    pallas_call x1, Pallas kernels: 127 us -> 118 us  [fock_build(): pl.pallas_call(fock_kernel, out_shape=jax.ShapeDtypeStruct((dens, n_out,...]
    unnamed x1, local copies, waits for them, and re-layouts: 0.12 us -> 2.18 us
    dot_general x1 -> x0, matrix products: 1.7 us -> none  [local_fock(): jnp.einsum('dmi,dli->mdl', orb_rows, orbitals, precision=PRECISE, preferr...]
where the time goes in v6:
time: 122 us; the launch traced here: 121 us
  Pallas kernels  118 us (97%)
  local copies, waits for them, and re-layouts  3.6 us (3%)
    pallas_call x1, Pallas kernels, fock_build(): pl.pallas_call(fock_kernel, out_shape=jax.ShapeDtypeStruct((dens, n_out,...  118 us

profile of v6, /device:TPU:0, one launch (start us, length us, event | category | flops | bytes accessed | tf_op | source)
XLA Modules:
  0.0 121.5 jit_solution(4908232163501816844)
XLA Ops:
  0.0 2.2 %copy.4.orb_ref = f32[4,384,80]{2,1,0:T(8,128)} copy(f32[4,384,80]{1,2,0:T(8,128)} %param.5) | data formatting | bytes 983040 | tf_op args[2]
  2.2 117.9 %fock_build.1 = f32[4,24,128]{2,1,0:T(8,128)} custom-call(f32[116,48,384]{2,1,0:T(8,128)} %ints_hbm.1, f32[4,384,80]{2,1,0:T(8,128)} %copy.4.orb_ref, f32[116,1856]{1,0:T(8,128)} %met_ref.1), custom_call_target="tpu_custom_call" | custom-call | tf_op jit(solution)/shard_map/fock_build/pallas_call | solution.py:332
  120.1 1.4 %slice_bitcast_fusion = f32[4,48,24]{1,2,0:T(8,128)} fusion(f32[4,24,128]{2,1,0:T(8,128)} %fock_build.1), kind=kLoop, calls=%fused_computation | loop fusion | bytes 36864 | tf_op jit(solution)/shard_map/transpose | solution.py:376

commit v7 on v6

--- a/solution.py
+++ b/solution.py
@@ -51,7 +51,7 @@
 
 
 def fock_kernel(ints_hbm, orb_ref, met_ref, out_ref,
-                ints, wide, terms, drows, met_blk, send, own, other, met, fit, kacc, kin, kpk, kall,
+                ints, wide, terms, orow, drows, met_blk, send, own, other, met, fit, kacc, kin, kpk, kall,
                 gam, gall, gsum, gpeer, gfit, fall, wb, jm, jt, jall,
                 ints_sem, met_send, met_recv, col_send, col_recv, pair_send, pair_recv, msg_send, msg_recv):
     z, y, x, core = mesh_pos()
@@ -90,13 +90,14 @@
     met[aux] = met_blk[:, pl.ds(pl.multiple_of(core * n_fit, n_fit), n_fit)].astype(BF16)
     ints[:, pl.ds(q_loc, LANES - q_loc)] = jnp.zeros((tiles, LANES - q_loc, m_pad, LANES), F32)
     flat = ints.reshape(tiles, LANES * m_pad, LANES)
-    dens, _, n_occ = orb_ref.shape
+    dens, n_occ, _ = orb_ref.shape
     drows[...] = jnp.zeros_like(drows)
     for d in range(dens):
-        for i, term in enumerate(split3(orb_ref[d].T)):
+        for i, term in enumerate(split3(orb_ref[d])):
             terms[i, pl.ds(d * n_occ, n_occ), :] = term
-        here = orb_ref[d, pl.ds(pl.multiple_of((x * 2 + core) * m_loc, m_loc), m_loc), :]
-        full = lax.dot_general(here, orb_ref[d], NT, precision=PRECISE, preferred_element_type=F32)
+        orow[d] = orb_ref[d].T
+        here = orow[d, pl.ds(pl.multiple_of((x * 2 + core) * m_loc, m_loc), m_loc), :]
+        full = jnp.dot(here, orb_ref[d], precision=PRECISE, preferred_element_type=F32)
         for t in range(tiles):
             drows[t, pl.ds(d, m_loc, stride=8), :] = full[:, t * LANES:(t + 1) * LANES]
     gam[...] = jnp.zeros_like(gam)
@@ -215,10 +216,10 @@
     await_bytes(twelve, met_recv.at[2])
     await_bytes(twelve, met_recv.at[3])
 
-    def col_step(c, carry, pump=False):
+    def col_step(c, carry, pump=(None,) * 4):
         def more(b):
-            if pump:
-                send_batch(c + 2, b)
+            if pump[b] is not None:
+                send_batch(*pump[b])
 
         more(0)
         await_bytes(own.at[c, pl.ds(1, n_src - 1)], col_recv.at[c])
@@ -238,10 +239,12 @@
                 more(3)
         return carry
 
-    lax.fori_loop(0, cols - 2, functools.partial(col_step, pump=True), 0)
+    col_step(0, 0, [(2, b) for b in range(4)])
+    col_step(1, 0, [(3, 0), None, (3, 1), None])
 
     await_bytes(fall.at[pl.ds(1, n_aux - 1)], msg_recv.at[2])
     wts = lax.dot_general(met_blk[...], jnp.concatenate([fall[a] for a in range(n_aux)], axis=1), NT, precision=PRECISE, preferred_element_type=F32)
+    send_batch(3, 2)
     for d in range(dens):
         wb[d] = jnp.broadcast_to(wts[:, d:d + 1], (LANES, LANES))
     jm[...] = jnp.zeros_like(jm)
@@ -257,7 +260,10 @@
                 jm[d // 2, pl.ds(pl.multiple_of((d % 2) * half_rows + 8 * g, 8), 8), pl.ds(LANES * t, LANES)] = acc[d * tiles + t]
         return carry
 
-    lax.fori_loop(0, groups, coul_group, 0)
+    lax.fori_loop(0, groups // 2, coul_group, 0)
+    send_batch(3, 3)
+    lax.fori_loop(groups // 2, groups, coul_group, 0)
+    send_batch(4, 0)
     for p in range(dens // 2):
         jt[p] = jm[p].T
 
@@ -268,7 +274,8 @@
                 push(jt.at[:, pl.ds(pl.multiple_of(to_aux * n_out, 8), n_out), :], jall.at[aux], msg_send.at[3], msg_recv.at[3], aux=to_aux)
     jall[aux] = jt[:, pl.ds(pl.multiple_of(aux * n_out, 8), n_out), :]
 
-    lax.fori_loop(cols - 2, cols, col_step, 0)
+    col_step(2, 0, [(4, 1), (4, 2), (4, 3), None])
+    lax.fori_loop(3, cols, col_step, 0)
 
     width = n_x * pad_rows
     mine = pl.multiple_of(core * width, width)
@@ -317,9 +324,9 @@
         await_bytes(met.at[pl.ds(0, n), upper], met_send.at[i])
 
 
-def fock_build(ints_blk, orbitals, metric_blk, n_aux):
+def fock_build(ints_blk, orb_cols, metric_blk, n_aux):
     q_loc, m_loc, n_bas = ints_blk.shape
-    dens, _, n_occ = orbitals.shape
+    dens, n_occ, _ = orb_cols.shape
     n_col = dens * n_occ
     n_x = n_bas // m_loc // 2
     chips = n_aux * n_x
@@ -338,6 +345,7 @@
             pltpu.VMEM((tiles, LANES, m_loc + 8, LANES), F32),
             pltpu.VMEM((n_col * (m_loc + 1), LANES), F32),
             pltpu.VMEM((3, n_col, n_bas), BF16),
+            pltpu.VMEM((dens, n_bas, n_occ), F32),
             pltpu.VMEM((tiles, 8 * m_loc, LANES), F32),
             pltpu.VMEM((LANES, 2 * n_fit), F32),
             pltpu.VMEM((chips, cols, m_loc, LANES), BF16),
@@ -363,7 +371,7 @@
         ],
         compiler_params=pltpu.CompilerParams(vmem_limit_bytes=62 * 1024 * 1024, collective_id=0, has_side_effects=True),
         name='fock_build',
-    )(ints_blk, orbitals, metric_blk)
+    )(ints_blk, orb_cols, metric_blk)
 
 
 def solution(mesh):
@@ -372,7 +380,7 @@
 
     def local_fock(ints_blk, metric_blk, orbitals):
         m_loc = ints_blk.shape[1]
-        out = fock_build(ints_blk, orbitals, metric_blk, n_aux)
+        out = fock_build(ints_blk, orbitals.transpose(0, 2, 1), metric_blk, n_aux)
         return out[:, :, :m_loc].transpose(0, 2, 1)
 
     return jax.shard_map(

time: 122 us -> 117 us (0.959)
  Pallas kernels: 118 us -> 115 us
  local copies, waits for them, and re-layouts: 3.6 us -> 1.42 us
    pallas_call x1, Pallas kernels: 118 us -> 115 us  [fock_build(): pl.pallas_call(fock_kernel, out_shape=jax.ShapeDtypeStruct((dens, n_out,...]
    unnamed x1 -> x0, local copies, waits for them, and re-layouts: 2.18 us -> none
where the time goes in v7:
time: 117 us
  Pallas kernels  115 us (98%)
  local copies, waits for them, and re-layouts  1.42 us (1%)
    pallas_call x1, Pallas kernels, fock_build(): pl.pallas_call(fock_kernel, out_shape=jax.ShapeDtypeStruct((dens, n_out,...  115 us

profile of v7, /device:TPU:0, one launch (start us, length us, event | category | flops | bytes accessed | tf_op | source)
XLA Modules:
  0.0 116.9 jit_solution(5723011263707687323)
XLA Ops:
  0.0 115.5 %fock_build.1 = f32[4,24,128]{2,1,0:T(8,128)} custom-call(f32[116,48,384]{2,1,0:T(8,128)} %ints_hbm.1, f32[4,80,384]{2,1,0:T(8,128)} %bitcast.3, f32[116,1856]{1,0:T(8,128)} %met_ref.1), custom_call_target="tpu_custom_call" | custom-call | tf_op jit(solution)/shard_map/fock_build/pallas_call | solution.py:339
  115.5 1.4 %slice_bitcast_fusion = f32[4,48,24]{1,2,0:T(8,128)} fusion(f32[4,24,128]{2,1,0:T(8,128)} %fock_build.1), kind=kLoop, calls=%fused_computation | loop fusion | bytes 36864 | tf_op jit(solution)/shard_map/transpose | solution.py:384

commit v8 on v7

--- a/solution.py
+++ b/solution.py
@@ -104,31 +104,64 @@
 
     upper, lower = pl.ds(0, half_rows), pl.ds(half_rows, half_rows)
 
-    def to_y(d, blk, half, n):
-        push(met.at[blk, half], met.at[blk, half], met_send.at[n], met_recv.at[n], aux=z * 4 + ys[d])
-
-    def to_z(d, blk, half, n):
-        push(met.at[blk, half], met.at[blk, half], met_send.at[n], met_recv.at[n], aux=zs[d] * 4 + y)
-
-    def gather_first():
-        for d in (1, 3, 2):
-            to_y(d, aux, upper, 0)
-            to_z(d, aux, lower, 1)
-        for d in (1, 3, 2):
-            to_z(d, aux, upper, 2)
-            to_y(d, aux, lower, 3)
-
-    def gather_second():
-        three = met.at[pl.ds(0, 3), upper]
-        await_bytes(three, met_recv.at[0])
-        await_bytes(three, met_recv.at[1])
-        for b in range(1, 4):
-            for d in (1, 3, 2):
-                to_z(d, z * 4 + ys[b], upper, 2)
-                to_y(d, zs[b] * 4 + y, lower, 3)
+    def along(axis, blk, start, n_rows, d, sem):
+        part = met.at[blk, pl.ds(start, n_rows)]
+        push(part, part, met_send.at[sem], met_recv.at[sem], aux=z * 4 + ys[d] if axis else zs[d] * 4 + y)
+
+    def spread(axis, blk, start, sem):
+        for d in (1, 3):
+            along(axis, blk, start, half_rows, d, sem)
+
+    def pass_on(axis, before, after, start, sem):
+        along(axis, before, start, half_rows // 2, 1, sem)
+        along(axis, after, start + half_rows // 2, half_rows // 2, 3, sem)
+
+    def at(dz, dy):
+        return zs[dz] * 4 + ys[dy]
+
+    blocks_in = (2, 2, 2, 2, 1, 1, 4, 4, 2, 2, 1, 1, 2, 2, 1, 1)
+
+    def got(sem):
+        await_bytes(met.at[pl.ds(0, blocks_in[sem]), upper], met_recv.at[sem])
+
+    def gather(stage):
+        low = half_rows
+        if stage == 0:
+            spread(1, aux, 0, 0)
+            spread(0, aux, low, 1)
+            spread(0, aux, 0, 2)
+            spread(1, aux, low, 3)
+        if stage == 1:
+            got(0)
+            got(1)
+            pass_on(1, at(0, 3), at(0, 1), 0, 4)
+            pass_on(0, at(3, 0), at(1, 0), low, 5)
+            for d in (1, 3):
+                spread(0, at(0, d), 0, 6)
+                spread(1, at(d, 0), low, 7)
+        if stage == 2:
+            got(4)
+            got(5)
+            spread(0, at(0, 2), 0, 8)
+            spread(1, at(2, 0), low, 9)
+            got(2)
+            got(3)
+            pass_on(0, at(3, 0), at(1, 0), 0, 10)
+            pass_on(1, at(0, 3), at(0, 1), low, 11)
+        if stage == 3:
+            got(6)
+            got(7)
+            for d in (1, 3):
+                pass_on(0, at(3, d), at(1, d), 0, 12)
+                pass_on(1, at(d, 3), at(d, 1), low, 13)
+        if stage == 4:
+            got(8)
+            got(9)
+            pass_on(0, at(3, 2), at(1, 2), 0, 14)
+            pass_on(1, at(2, 3), at(2, 1), low, 15)
 
     pl.semaphore_wait(barrier, n_src)
-    gather_first()
+    gather(0)
     for g in range(groups):
         for copy in copies[g]:
             copy.wait()
@@ -151,8 +184,8 @@
             return carry
 
         lax.fori_loop(0, 4, pair_step, 0)
-        if g == 2:
-            gather_second()
+        if g in (1, 2, 4, 5):
+            gather(g if g < 3 else g - 1)
 
     def narrow(c):
         def one(to, carry):
@@ -177,13 +210,12 @@
     for c in range(cols):
         own[c, me] = send[me, c]
 
-    for b in range(4):
-        send_batch(1, b)
-
     await_bytes(gall.at[pl.ds(1, n_src - 1)], msg_recv.at[0])
     for a in range(n_aux):
         gsum[a] = (gall[n_x * a] + gall[n_x * a + 1]) + (gall[n_x * a + 2] + gall[n_x * a + 3])
-    push(gsum, gpeer, msg_send.at[1], msg_recv.at[1], core=1 - core).wait()
+    swap = push(gsum, gpeer, msg_send.at[1], msg_recv.at[1], core=1 - core)
+    send_batch(1, 0)
+    swap.wait()
 
     def times_met(blocks):
         return lax.dot_general(jnp.concatenate(blocks, axis=1), met_blk[...], NT, precision=PRECISE, preferred_element_type=F32)
@@ -194,6 +226,7 @@
             if dz or dy:
                 push(gfit, fall.at[aux], msg_send.at[2], msg_recv.at[2], aux=zs[dz] * 4 + ys[dy])
     fall[aux] = gfit[...]
+    send_batch(1, 1)
 
     fit[...] = jnp.zeros_like(fit)
     kacc[...] = jnp.zeros_like(kacc)
@@ -212,9 +245,8 @@
                 start = pl.multiple_of((side * n_x + b) * pad_rows, pad_rows)
                 fit[pl.ds(start, m_loc), pl.ds(n * tile, tile)] = tot[b * m_loc:(b + 1) * m_loc]
 
-    twelve = met.at[pl.ds(0, 12), upper]
-    await_bytes(twelve, met_recv.at[2])
-    await_bytes(twelve, met_recv.at[3])
+    for sem in range(10, 16):
+        got(sem)
 
     def col_step(c, carry, pump=(None,) * 4):
         def more(b):
@@ -239,12 +271,12 @@
                 more(3)
         return carry
 
-    col_step(0, 0, [(2, b) for b in range(4)])
-    col_step(1, 0, [(3, 0), None, (3, 1), None])
+    col_step(0, 0, [(1, 2), (1, 3), (2, 0), (2, 1)])
+    col_step(1, 0, [(2, 2), (2, 3), (3, 0), None])
 
     await_bytes(fall.at[pl.ds(1, n_aux - 1)], msg_recv.at[2])
     wts = lax.dot_general(met_blk[...], jnp.concatenate([fall[a] for a in range(n_aux)], axis=1), NT, precision=PRECISE, preferred_element_type=F32)
-    send_batch(3, 2)
+    send_batch(3, 1)
     for d in range(dens):
         wb[d] = jnp.broadcast_to(wts[:, d:d + 1], (LANES, LANES))
     jm[...] = jnp.zeros_like(jm)
@@ -261,9 +293,9 @@
         return carry
 
     lax.fori_loop(0, groups // 2, coul_group, 0)
+    send_batch(3, 2)
+    lax.fori_loop(groups // 2, groups, coul_group, 0)
     send_batch(3, 3)
-    lax.fori_loop(groups // 2, groups, coul_group, 0)
-    send_batch(4, 0)
     for p in range(dens // 2):
         jt[p] = jm[p].T
 
@@ -274,7 +306,7 @@
                 push(jt.at[:, pl.ds(pl.multiple_of(to_aux * n_out, 8), n_out), :], jall.at[aux], msg_send.at[3], msg_recv.at[3], aux=to_aux)
     jall[aux] = jt[:, pl.ds(pl.multiple_of(aux * n_out, 8), n_out), :]
 
-    col_step(2, 0, [(4, 1), (4, 2), (4, 3), None])
+    col_step(2, 0, [(4, 0), (4, 1), (4, 2), (4, 3)])
     lax.fori_loop(3, cols, col_step, 0)
 
     width = n_x * pad_rows
@@ -320,7 +352,7 @@
     await_bytes(fall.at[pl.ds(1, n_aux - 1)], msg_send.at[2])
     await_bytes(jall.at[pl.ds(1, n_aux - 1)], msg_send.at[3])
     await_bytes(kall.at[pl.ds(1, n_src - 1)], msg_send.at[5])
-    for i, n in enumerate((3, 3, 12, 12)):
+    for i, n in enumerate(blocks_in):
         await_bytes(met.at[pl.ds(0, n), upper], met_send.at[i])
 
 
@@ -367,7 +399,7 @@
             pltpu.VMEM((dens // 2, LANES, n_bas), F32),
             pltpu.VMEM((dens // 2, n_bas, LANES), F32),
             pltpu.VMEM((n_aux, dens // 2, n_out, LANES), F32),
-            dma((m_loc // 8, tiles)), dma((4,)), dma((4,)), dma((cols,)), dma((cols,)), dma((cols,)), dma((cols,)), dma((6,)), dma((6,)),
+            dma((m_loc // 8, tiles)), dma((16,)), dma((16,)), dma((cols,)), dma((cols,)), dma((cols,)), dma((cols,)), dma((6,)), dma((6,)),
         ],
         compiler_params=pltpu.CompilerParams(vmem_limit_bytes=62 * 1024 * 1024, collective_id=0, has_side_effects=True),
         name='fock_build',

time: 117 us -> 111 us (0.949)
  Pallas kernels: 115 us -> 109 us
    pallas_call x1, Pallas kernels: 115 us -> 109 us  [fock_build(): pl.pallas_call(fock_kernel, out_shape=jax.ShapeDtypeStruct((dens, n_out,...]
where the time goes in v8:
time: 111 us
  Pallas kernels  109 us (98%)
  local copies, waits for them, and re-layouts  1.42 us (1%)
    pallas_call x1, Pallas kernels, fock_build(): pl.pallas_call(fock_kernel, out_shape=jax.ShapeDtypeStruct((dens, n_out,...  109 us

profile of v8, /device:TPU:0, one launch (start us, length us, event | category | flops | bytes accessed | tf_op | source)
XLA Modules:
  0.0 110.7 jit_solution(12563545906305300748)
XLA Ops:
  0.0 109.3 %fock_build.1 = f32[4,24,128]{2,1,0:T(8,128)} custom-call(f32[116,48,384]{2,1,0:T(8,128)} %ints_hbm.1, f32[4,80,384]{2,1,0:T(8,128)} %bitcast.3, f32[116,1856]{1,0:T(8,128)} %met_ref.1), custom_call_target="tpu_custom_call" | custom-call | tf_op jit(solution)/shard_map/fock_build/pallas_call | solution.py:371
  109.3 1.4 %slice_bitcast_fusion = f32[4,48,24]{1,2,0:T(8,128)} fusion(f32[4,24,128]{2,1,0:T(8,128)} %fock_build.1), kind=kLoop, calls=%fused_computation | loop fusion | bytes 36864 | tf_op jit(solution)/shard_map/transpose | solution.py:416

commit v9 on v8

--- a/solution.py
+++ b/solution.py
@@ -203,10 +203,10 @@
         for to_aux, to_x in batch(zs, ys, xs, b):
             push(gam, gall.at[me], msg_send.at[0], msg_recv.at[0], aux=to_aux, x=to_x)
     gall[me] = gam[...]
-    for b in range(4):
-        send_batch(0, b)
+    send_batch(0, 0)
     for c in range(1, cols):
         narrow(c)
+    send_batch(0, 1)
     for c in range(cols):
         own[c, me] = send[me, c]
 
@@ -214,7 +214,7 @@
     for a in range(n_aux):
         gsum[a] = (gall[n_x * a] + gall[n_x * a + 1]) + (gall[n_x * a + 2] + gall[n_x * a + 3])
     swap = push(gsum, gpeer, msg_send.at[1], msg_recv.at[1], core=1 - core)
-    send_batch(1, 0)
+    send_batch(0, 2)
     swap.wait()
 
     def times_met(blocks):
@@ -226,6 +226,8 @@
             if dz or dy:
                 push(gfit, fall.at[aux], msg_send.at[2], msg_recv.at[2], aux=zs[dz] * 4 + ys[dy])
     fall[aux] = gfit[...]
+    send_batch(0, 3)
+    send_batch(1, 0)
     send_batch(1, 1)
 
     fit[...] = jnp.zeros_like(fit)

time: 111 us -> 112 us (level)
  no operation moved by 1% of the time
where the time goes in v9:
time: 112 us
  Pallas kernels  110 us (98%)
  local copies, waits for them, and re-layouts  1.42 us (1%)
    pallas_call x1, Pallas kernels, fock_build(): pl.pallas_call(fock_kernel, out_shape=jax.ShapeDtypeStruct((dens, n_out,...  110 us

profile of v9, /device:TPU:0, one launch (start us, length us, event | category | flops | bytes accessed | tf_op | source)
XLA Modules:
  0.0 111.7 jit_solution(2500407393138840113)
XLA Ops:
  0.0 110.2 %fock_build.1 = f32[4,24,128]{2,1,0:T(8,128)} custom-call(f32[116,48,384]{2,1,0:T(8,128)} %ints_hbm.1, f32[4,80,384]{2,1,0:T(8,128)} %bitcast.3, f32[116,1856]{1,0:T(8,128)} %met_ref.1), custom_call_target="tpu_custom_call" | custom-call | tf_op jit(solution)/shard_map/fock_build/pallas_call | solution.py:373
  110.2 1.4 %slice_bitcast_fusion = f32[4,48,24]{1,2,0:T(8,128)} fusion(f32[4,24,128]{2,1,0:T(8,128)} %fock_build.1), kind=kLoop, calls=%fused_computation | loop fusion | bytes 36864 | tf_op jit(solution)/shard_map/transpose | solution.py:418
